TPU v7x, 32 devices: a whole 2x2x4 slice. The times are simulated.
32 devices in a mesh: tm: 2 (over x), src: 16 (over z, y, core).
Axes of the slice: x: 2, y: 2, z: 4, core: 2. Of those that a mesh axis runs over, the one named last changes fastest.
Arguments:
- design: float32 [16, 524288], P(None, ('tm', 'src')), may hold values from -2 to 2
- unit_index: int32 [524288], P(('tm', 'src')), may hold values from 0 to 255, as said below
- residual: float32 [524288], P(('tm', 'src')), may hold values from -6 to 6
- weight: float32 [524288], P(('tm', 'src')), may hold values from 0.25 to 4
- obs_count: int32 [32], P(('tm', 'src')), may hold values from 1 to 16384, as said below
- damping: float32 [256], P(('tm', 'src')), may hold values from 1 to 10
Outputs:
- solution: float32 [16, 256], P(None, ('tm', 'src'))
- misfit: float32 [], replicated
Inputs may be any that keep to these rules, and one draw needn't show every extreme that they name: `unit_index`: an observation on a device of tm index g names a unit in [g * 128, (g + 1) * 128). `obs_count`: some device has all 16384 slots live.
All inputs are finite; a program needn't handle non-finite values.
Results may differ from a plain program's by a relative error of at most 0.0003.
Values sent between devices are 32-bit elements; how exact they have to be, the bound alone decides.
A program may use at most 64 MiB of HBM per device.

v0:
```python
import functools

import jax
import jax.numpy as jnp
from jax import lax
from jax.experimental import pallas as pl
from jax.experimental.pallas import tpu as pltpu
from jax.sharding import PartitionSpec as P

WIDTH = 16
HALF = 8
PAIRS = WIDTH * (WIDTH + 1) // 2
ROWS = PAIRS + WIDTH
LANES = 128
FOLD = 4


def pair_row(i, j):
    k = (j - i) % WIDTH
    if k > HALF or (k == HALF and i >= HALF):
        i, j = j, i
        k = (j - i) % WIDTH
    return k * WIDTH + i


def stacked_rows(d0, d1, w, wr):
    w0, w1 = d0 * w, d1 * w
    rows = [d0 * w0, d1 * w1]
    sub = lax.broadcasted_iota(jnp.int32, d0.shape, 0)
    for k in range(1, HALF):
        r0 = pltpu.roll(w0, HALF - k, 0)
        r1 = pltpu.roll(w1, HALF - k, 0)
        low = sub < HALF - k
        rows.append(d0 * jnp.where(low, r0, r1))
        rows.append(d1 * jnp.where(low, r1, r0))
    rows.append(d0 * w1)
    rows.append(d0 * wr)
    rows.append(d1 * wr)
    return rows


def rsqrt(value):
    guess = lax.rsqrt(value)
    return guess * (1.5 - 0.5 * value * guess * guess)


def solve(entry, rhs, damping):
    a = {}
    for i in range(WIDTH):
        for j in range(i + 1):
            a[i, j] = entry(i, j)
        a[i, i] = a[i, i] + damping
    b = [rhs(i) for i in range(WIDTH)]
    inverse, forward = [], []
    for j in range(WIDTH):
        inv = rsqrt(a[j, j])
        inverse.append(inv)
        for i in range(j + 1, WIDTH):
            a[i, j] = a[i, j] * inv
        y = b[j] * inv
        forward.append(y)
        for i in range(j + 1, WIDTH):
            b[i] = b[i] - a[i, j] * y
            for k in range(j + 1, i + 1):
                a[i, k] = a[i, k] - a[i, j] * a[k, j]
    run = list(forward)
    x = [None] * WIDTH
    for i in reversed(range(WIDTH)):
        x[i] = run[i] * inverse[i]
        for k in range(i):
            run[k] = run[k] - a[i, k] * x[i]
    return x, forward


def far_first(n):
    q = max(n // 4, 1)
    order = []
    for i in range(q):
        order += [3 * q + i, q + i]
    order += list(range(2 * q, 3 * q)) + list(range(1, q))
    return [p for p in dict.fromkeys(order) if 0 < p < n]


def each(pairs, body, start):
    if len(pairs) <= 32:
        for dt, dp in pairs:
            start = body(dt, dp, start)
        return start
    n_src = max(dp for _, dp in pairs) + 1
    return lax.fori_loop(
        1, len(pairs) + 1, lambda i, c: body(i // n_src, i % n_src, c), start
    )


def kernel(
    n_tm, n_src, chunk,
    count_hbm, design_hbm, unit_hbm, resid_hbm, weight_hbm, damp_hbm,
    x_ref, misfit_ref,
    count_ref, design_ref, unit_ref, resid_ref, weight_ref, damp_ref,
    acc, extra, part, tail, got, got_tail, summed, spread, mine, heard,
    load, small, send_a, recv_a, send_b, recv_b,
):
    tm, src = lax.axis_index("tm"), lax.axis_index("src")
    n_all = n_tm * n_src
    me = tm * n_src + src
    own = damp_ref.shape[1]
    units = own * n_src
    slots = design_ref.shape[1]
    turns = slots // chunk
    order = far_first(n_src)
    near = [(0, p) for p in order]
    everyone = [(dt, p) for dt in range(n_tm - 1, 0, -1) for p in order + [0]] + near

    arrays = (
        (design_hbm, design_ref), (unit_hbm, unit_ref),
        (resid_hbm, resid_ref), (weight_hbm, weight_ref),
    )

    def fetch(step, which):
        far, here = arrays[which]
        cols = pl.ds(pl.multiple_of(step * chunk, chunk), chunk)
        return pltpu.make_async_copy(far.at[:, cols], here.at[:, cols], load.at[step, which])

    count_copy = pltpu.make_async_copy(count_hbm, count_ref, small.at[0])
    damp_copy = pltpu.make_async_copy(damp_hbm, damp_ref, small.at[1])
    count_copy.start()
    for which in range(4):
        fetch(0, which).start()
    for step in range(1, turns):
        for which in range(4):
            fetch(step, which).start()
    damp_copy.start()

    def at(dt, dp):
        return {"tm": (tm + dt) % n_tm, "src": (src + dp) % n_src}

    barrier = pltpu.get_barrier_semaphore()

    def greet(dt, dp, c):
        pl.semaphore_signal(
            barrier, inc=1, device_id=at(dt, dp), device_id_type=pl.DeviceIdType.MESH
        )
        return c

    each(everyone, greet, 0)

    first_unit = tm * units
    zero = jnp.zeros((1, LANES), jnp.float32)
    count_copy.wait()
    count = count_ref[0]

    def accumulate(step, carry):
        chi, total = carry
        for which in range(4):
            fetch(step, which).wait()
        begin = pl.multiple_of(step * chunk, chunk)
        cols = pl.ds(begin, chunk)
        w = weight_ref[:, cols]
        live = begin + lax.broadcasted_iota(jnp.int32, w.shape, 1) < count
        w = jnp.where(live, w, 0.0)
        r = resid_ref[:, cols]
        wr = w * r
        rows = stacked_rows(design_ref[0:HALF, cols], design_ref[HALF:WIDTH, cols], w, wr)
        x = jnp.concatenate(rows, axis=0)
        high = x.astype(jnp.bfloat16).astype(jnp.float32)
        lhs = jnp.concatenate([high, x - high], axis=0).astype(jnp.bfloat16)
        unit = unit_ref[:, cols] - first_unit
        hot = lax.broadcasted_iota(jnp.int32, (units, chunk), 0) == unit
        hot = jnp.where(hot, 1.0, 0.0).astype(jnp.bfloat16)
        acc[...] += lax.dot_general(
            lhs, hot, (((1,), (1,)), ((), ())), preferred_element_type=jnp.float32
        )
        wrr = wr * r
        for t in range(chunk // LANES):
            chi = chi + wrr[:, t * LANES:(t + 1) * LANES]
            total = total + w[:, t * LANES:(t + 1) * LANES]
        return chi, total

    acc[...] = jnp.zeros_like(acc)
    chi, total = lax.fori_loop(0, turns, accumulate, (zero, zero))

    sums = acc[0:ROWS] + acc[ROWS:2 * ROWS]
    left = jnp.concatenate(
        [sums[LANES:ROWS], jnp.zeros((2 * LANES - ROWS, units), jnp.float32)], axis=0
    )
    extra[...] = jnp.transpose(left)
    part[...] = jnp.transpose(sums[0:LANES]).reshape(n_src, own, LANES)
    packed = extra[pl.ds(0, units // FOLD, stride=FOLD), :]
    for b in range(1, FOLD):
        packed = packed + pltpu.roll(
            extra[pl.ds(b, units // FOLD, stride=FOLD), :], b * (LANES // FOLD), 1
        )
    tail[...] = packed.reshape(n_src, own // FOLD, LANES)

    pl.semaphore_wait(barrier, n_all - 1)

    def exchange(peer, slot, which):
        mine_of, theirs = ((part, got), (tail, got_tail))[which]
        return pltpu.make_async_remote_copy(
            src_ref=mine_of.at[peer], dst_ref=theirs.at[slot],
            send_sem=send_a.at[which, peer], recv_sem=recv_a.at[which, slot],
            device_id={"tm": tm, "src": peer}, device_id_type=pl.DeviceIdType.MESH,
        )

    def send_one(dt, dp, c):
        to = (src + dp) % n_src
        exchange(to, src, 0).start()
        exchange(to, src, 1).start()
        return c

    each(near, send_one, 0)

    def take_one(dt, dp, carry):
        frm = (src - dp + n_src) % n_src
        exchange(frm, frm, 0).wait_recv()
        exchange(frm, frm, 1).wait_recv()
        return carry[0] + got[frm], carry[1] + got_tail[frm]

    whole, ends = each(list(reversed(near)), take_one, (part[src], tail[src]))
    for a in range(own // FOLD):
        for b in range(FOLD):
            row = ends[a:a + 1]
            spread[pl.ds(a * FOLD + b, 1), :] = (
                pltpu.roll(row, LANES - b * (LANES // FOLD), 1) if b else row
            )
    summed[0:LANES, :] = jnp.transpose(whole)
    summed[LANES:2 * LANES, :] = jnp.transpose(spread[...])

    damp_copy.wait()
    damping = damp_ref[...]
    x, forward = solve(
        lambda i, j: summed[pl.ds(pair_row(i, j), 1), :],
        lambda i: summed[pl.ds(PAIRS + i, 1), :],
        damping,
    )
    terms = jnp.zeros_like(damping)
    squared = jnp.zeros_like(damping)
    for i in range(WIDTH):
        terms = terms + forward[i] * forward[i]
        squared = squared + x[i] * x[i]
    terms = terms + damping * squared
    chi = chi - jnp.concatenate([terms, jnp.zeros((1, LANES - own), jnp.float32)], axis=1)
    lane = lax.broadcasted_iota(jnp.int32, (1, LANES), 1)
    front = lane < LANES // 2
    chi = chi + pltpu.roll(chi, LANES // 2, 1)
    total = total + pltpu.roll(total, LANES // 2, 1)
    mine[...] = jnp.where(front, chi, total)

    def tell(dt, dp):
        to = ((tm + dt) % n_tm) * n_src + (src + dp) % n_src
        return pltpu.make_async_remote_copy(
            src_ref=mine, dst_ref=heard.at[me],
            send_sem=send_b.at[to], recv_sem=recv_b.at[me],
            device_id=at(dt, dp), device_id_type=pl.DeviceIdType.MESH,
        )

    def tell_one(dt, dp, c):
        tell(dt, dp).start()
        return c

    each(everyone, tell_one, 0)

    x_ref[...] = jnp.transpose(jnp.concatenate(x, axis=0))

    def hear_one(dt, dp, value):
        frm = ((tm + dt) % n_tm) * n_src + (src + dp) % n_src
        pltpu.make_async_remote_copy(
            src_ref=mine, dst_ref=heard.at[frm],
            send_sem=send_b.at[frm], recv_sem=recv_b.at[frm],
            device_id=at(dt, dp), device_id_type=pl.DeviceIdType.MESH,
        ).wait_recv()
        return value + heard[frm]

    def drain_a(dt, dp, c):
        to = (src + dp) % n_src
        exchange(to, src, 0).wait_send()
        exchange(to, src, 1).wait_send()
        return c

    each(near, drain_a, 0)
    both = each(list(reversed(everyone)), hear_one, mine[...])
    chi_all = jnp.sum(jnp.where(front, both, 0.0), axis=1, keepdims=True)
    total_all = jnp.sum(jnp.where(front, 0.0, both), axis=1, keepdims=True)
    misfit_ref[...] = chi_all / total_all

    def drain_b(dt, dp, c):
        tell(dt, dp).wait_send()
        return c

    each(everyone, drain_b, 0)


def hand_on(x_ref, misfit_ref, x_out, misfit_out):
    x_out[...] = x_ref[...]
    misfit_out[...] = misfit_ref[...]


def solution(mesh):
    n_tm, n_src = mesh.shape["tm"], mesh.shape["src"]
    n_all = n_tm * n_src

    def on_device(design, unit_index, residual, weight, obs_count, damping):
        own = damping.shape[0]
        units = own * n_src
        slots = design.shape[1]
        chunk = 8192 if slots % 8192 == 0 else LANES
        turns = slots // chunk
        anywhere = pl.BlockSpec(memory_space=pl.ANY)
        vmem = pl.BlockSpec(memory_space=pltpu.VMEM)
        x, misfit = pl.pallas_call(
            functools.partial(kernel, n_tm, n_src, chunk),
            out_shape=(
                jax.ShapeDtypeStruct((own, WIDTH), jnp.float32),
                jax.ShapeDtypeStruct((1, 1), jnp.float32),
            ),
            in_specs=[anywhere] * 6,
            out_specs=(vmem, vmem),
            scratch_shapes=[
                pltpu.SMEM((1,), jnp.int32),
                pltpu.VMEM((WIDTH, slots), jnp.float32),
                pltpu.VMEM((1, slots), jnp.int32),
                pltpu.VMEM((1, slots), jnp.float32),
                pltpu.VMEM((1, slots), jnp.float32),
                pltpu.VMEM((1, own), jnp.float32),
                pltpu.VMEM((2 * ROWS, units), jnp.float32),
                pltpu.VMEM((units, LANES), jnp.float32),
                pltpu.VMEM((n_src, own, LANES), jnp.float32),
                pltpu.VMEM((n_src, own // FOLD, LANES), jnp.float32),
                pltpu.VMEM((n_src, own, LANES), jnp.float32),
                pltpu.VMEM((n_src, own // FOLD, LANES), jnp.float32),
                pltpu.VMEM((2 * LANES, own), jnp.float32),
                pltpu.VMEM((own, LANES), jnp.float32),
                pltpu.VMEM((1, LANES), jnp.float32),
                pltpu.VMEM((n_all, 1, LANES), jnp.float32),
                pltpu.SemaphoreType.DMA((turns, 4)),
                pltpu.SemaphoreType.DMA((2,)),
                pltpu.SemaphoreType.DMA((2, n_src)),
                pltpu.SemaphoreType.DMA((2, n_src)),
                pltpu.SemaphoreType.DMA((n_all,)),
                pltpu.SemaphoreType.DMA((n_all,)),
            ],
            compiler_params=pltpu.CompilerParams(collective_id=0, has_side_effects=True),
            name="calibrate",
        )(
            obs_count,
            design,
            unit_index.reshape(1, slots),
            residual.reshape(1, slots),
            weight.reshape(1, slots),
            damping.reshape(1, own),
        )
        x, misfit = pl.pallas_call(
            hand_on,
            out_shape=(
                jax.ShapeDtypeStruct((own, WIDTH), jnp.float32),
                jax.ShapeDtypeStruct((1, 1), jnp.float32),
            ),
            in_specs=[vmem, vmem],
            out_specs=(vmem, vmem),
            name="hand_on",
        )(x, misfit)
        return x.T, misfit.reshape(())

    both = ("tm", "src")
    return jax.shard_map(
        on_device,
        mesh=mesh,
        in_specs=(P(None, both), P(both), P(both), P(both), P(both), P(both)),
        out_specs=(P(None, both), P()),
        check_vma=False,
    )
```

profile of v0, /device:TPU:0, one launch (start us, length us, event | category | flops | bytes accessed | tf_op | source)
XLA Modules:
  0.0 21.9 jit_solution(12541056939466410961)
XLA Ops:
  1.3 18.7 %calibrate.1 = (f32[8,16]{1,0:T(8,128)}, f32[1,1]{1,0:T(1,128)}) custom-call(s32[1]{0:T(128)S(6)} %copy.8.count_hbm, f32[16,16384]{1,0:T(8,128)} %design_hbm.1, s32[1,16384]{1,0:T(1,128)} %bitcast.6, f32[1,16384]{1,0:T(1,128)} %bitcast.7, f32[1,16384]{1,0:T(1,128)} %bitcast.8, f32[1,8]{1,0:T(1,128)} %bitcast.9), custom_call_target="tpu_custom_call" | custom-call | tf_op jit(solution)/shard_map/calibrate/pallas_call | solution.py:310
  20.0 1.9 %hand_on.1 = (f32[8,16]{1,0:T(8,128)}, f32[1,1]{1,0:T(1,128)}) custom-call(f32[8,16]{1,0:T(8,128)} %get-tuple-element.6.x_ref, f32[1,1]{1,0:T(1,128)} %get-tuple-element.7.misfit_ref), custom_call_target="tpu_custom_call" | custom-call | tf_op jit(solution)/shard_map/hand_on/pallas_call | solution.py:352
where the time goes:
time: 22.1 us; the launch traced here: 21.9 us
  Pallas kernels  20.6 us (93%)
  between operations  1.29 us (6%)
    pallas_call x1, Pallas kernels, on_device(): pl.pallas_call(functools.partial(kernel, n_tm, n_src, chunk), out_shape=(...  18.7 us
    pallas_call x1, Pallas kernels, on_device(): pl.pallas_call(hand_on, out_shape=(jax.ShapeDtypeStruct((own, WIDTH), jnp...  1.9 us

commit v1 on v0

--- a/solution.py
+++ b/solution.py
@@ -95,9 +95,9 @@
 def kernel(
     n_tm, n_src, chunk,
     count_hbm, design_hbm, unit_hbm, resid_hbm, weight_hbm, damp_hbm,
-    x_ref, misfit_ref,
+    out_ref,
     count_ref, design_ref, unit_ref, resid_ref, weight_ref, damp_ref,
-    acc, extra, part, tail, got, got_tail, summed, spread, mine, heard,
+    acc, extra, part, got, summed, spread, mine, heard,
     load, small, send_a, recv_a, send_b, recv_b,
 ):
     tm, src = lax.axis_index("tm"), lax.axis_index("src")
@@ -184,39 +184,32 @@
         [sums[LANES:ROWS], jnp.zeros((2 * LANES - ROWS, units), jnp.float32)], axis=0
     )
     extra[...] = jnp.transpose(left)
-    part[...] = jnp.transpose(sums[0:LANES]).reshape(n_src, own, LANES)
+    part[:, 0:own, :] = jnp.transpose(sums[0:LANES]).reshape(n_src, own, LANES)
     packed = extra[pl.ds(0, units // FOLD, stride=FOLD), :]
     for b in range(1, FOLD):
         packed = packed + pltpu.roll(
             extra[pl.ds(b, units // FOLD, stride=FOLD), :], b * (LANES // FOLD), 1
         )
-    tail[...] = packed.reshape(n_src, own // FOLD, LANES)
+    part[:, own:, :] = packed.reshape(n_src, own // FOLD, LANES)
 
     pl.semaphore_wait(barrier, n_all - 1)
-
-    def exchange(peer, slot, which):
-        mine_of, theirs = ((part, got), (tail, got_tail))[which]
-        return pltpu.make_async_remote_copy(
-            src_ref=mine_of.at[peer], dst_ref=theirs.at[slot],
-            send_sem=send_a.at[which, peer], recv_sem=recv_a.at[which, slot],
-            device_id={"tm": tm, "src": peer}, device_id_type=pl.DeviceIdType.MESH,
-        )
 
     def send_one(dt, dp, c):
         to = (src + dp) % n_src
-        exchange(to, src, 0).start()
-        exchange(to, src, 1).start()
+        pltpu.make_async_remote_copy(
+            src_ref=part.at[to], dst_ref=got.at[src], send_sem=send_a, recv_sem=recv_a,
+            device_id={"tm": tm, "src": to}, device_id_type=pl.DeviceIdType.MESH,
+        ).start()
         return c
 
     each(near, send_one, 0)
-
-    def take_one(dt, dp, carry):
-        frm = (src - dp + n_src) % n_src
-        exchange(frm, frm, 0).wait_recv()
-        exchange(frm, frm, 1).wait_recv()
-        return carry[0] + got[frm], carry[1] + got_tail[frm]
-
-    whole, ends = each(list(reversed(near)), take_one, (part[src], tail[src]))
+    got[src] = part[src]
+    others = got.at[pl.ds(0, n_src - 1)]
+    pltpu.make_async_copy(others, others, recv_a).wait()
+    both = got[0]
+    for p in range(1, n_src):
+        both = both + got[p]
+    whole, ends = both[0:own], both[own:]
     for a in range(own // FOLD):
         for b in range(FOLD):
             row = ends[a:a + 1]
@@ -245,54 +238,32 @@
     chi = chi + pltpu.roll(chi, LANES // 2, 1)
     total = total + pltpu.roll(total, LANES // 2, 1)
     mine[...] = jnp.where(front, chi, total)
-
-    def tell(dt, dp):
-        to = ((tm + dt) % n_tm) * n_src + (src + dp) % n_src
-        return pltpu.make_async_remote_copy(
-            src_ref=mine, dst_ref=heard.at[me],
-            send_sem=send_b.at[to], recv_sem=recv_b.at[me],
+    heard[me] = mine[...]
+
+    def tell_one(dt, dp, c):
+        pltpu.make_async_remote_copy(
+            src_ref=mine, dst_ref=heard.at[me], send_sem=send_b, recv_sem=recv_b,
             device_id=at(dt, dp), device_id_type=pl.DeviceIdType.MESH,
-        )
-
-    def tell_one(dt, dp, c):
-        tell(dt, dp).start()
+        ).start()
         return c
 
     each(everyone, tell_one, 0)
 
-    x_ref[...] = jnp.transpose(jnp.concatenate(x, axis=0))
-
-    def hear_one(dt, dp, value):
-        frm = ((tm + dt) % n_tm) * n_src + (src + dp) % n_src
-        pltpu.make_async_remote_copy(
-            src_ref=mine, dst_ref=heard.at[frm],
-            send_sem=send_b.at[frm], recv_sem=recv_b.at[frm],
-            device_id=at(dt, dp), device_id_type=pl.DeviceIdType.MESH,
-        ).wait_recv()
-        return value + heard[frm]
-
-    def drain_a(dt, dp, c):
-        to = (src + dp) % n_src
-        exchange(to, src, 0).wait_send()
-        exchange(to, src, 1).wait_send()
-        return c
-
-    each(near, drain_a, 0)
-    both = each(list(reversed(everyone)), hear_one, mine[...])
+    out_ref[:, 0:WIDTH] = jnp.transpose(jnp.concatenate(x, axis=0))
+    sent = part.at[pl.ds(0, n_src - 1)]
+    pltpu.make_async_copy(sent, sent, send_a).wait()
+    told = heard.at[pl.ds(0, n_all - 1)]
+    pltpu.make_async_copy(told, told, recv_b).wait()
+    both = jnp.sum(heard[...].reshape(n_all, LANES), axis=0, keepdims=True)
     chi_all = jnp.sum(jnp.where(front, both, 0.0), axis=1, keepdims=True)
     total_all = jnp.sum(jnp.where(front, 0.0, both), axis=1, keepdims=True)
-    misfit_ref[...] = chi_all / total_all
-
-    def drain_b(dt, dp, c):
-        tell(dt, dp).wait_send()
-        return c
-
-    each(everyone, drain_b, 0)
-
-
-def hand_on(x_ref, misfit_ref, x_out, misfit_out):
-    x_out[...] = x_ref[...]
-    misfit_out[...] = misfit_ref[...]
+    out_ref[0:1, WIDTH:WIDTH + 1] = chi_all / total_all
+    pltpu.make_async_copy(told, told, send_b).wait()
+
+
+def hand_on(both_ref, x_out, misfit_out):
+    x_out[...] = both_ref[:, 0:WIDTH]
+    misfit_out[...] = both_ref[0:1, WIDTH:WIDTH + 1]
 
 
 def solution(mesh):
@@ -307,14 +278,11 @@
         turns = slots // chunk
         anywhere = pl.BlockSpec(memory_space=pl.ANY)
         vmem = pl.BlockSpec(memory_space=pltpu.VMEM)
-        x, misfit = pl.pallas_call(
+        result = pl.pallas_call(
             functools.partial(kernel, n_tm, n_src, chunk),
-            out_shape=(
-                jax.ShapeDtypeStruct((own, WIDTH), jnp.float32),
-                jax.ShapeDtypeStruct((1, 1), jnp.float32),
-            ),
+            out_shape=pltpu.VMEM((own, LANES), jnp.float32),
             in_specs=[anywhere] * 6,
-            out_specs=(vmem, vmem),
+            out_specs=vmem,
             scratch_shapes=[
                 pltpu.SMEM((1,), jnp.int32),
                 pltpu.VMEM((WIDTH, slots), jnp.float32),
@@ -324,20 +292,18 @@
                 pltpu.VMEM((1, own), jnp.float32),
                 pltpu.VMEM((2 * ROWS, units), jnp.float32),
                 pltpu.VMEM((units, LANES), jnp.float32),
-                pltpu.VMEM((n_src, own, LANES), jnp.float32),
-                pltpu.VMEM((n_src, own // FOLD, LANES), jnp.float32),
-                pltpu.VMEM((n_src, own, LANES), jnp.float32),
-                pltpu.VMEM((n_src, own // FOLD, LANES), jnp.float32),
+                pltpu.VMEM((n_src, own + own // FOLD, LANES), jnp.float32),
+                pltpu.VMEM((n_src, own + own // FOLD, LANES), jnp.float32),
                 pltpu.VMEM((2 * LANES, own), jnp.float32),
                 pltpu.VMEM((own, LANES), jnp.float32),
                 pltpu.VMEM((1, LANES), jnp.float32),
                 pltpu.VMEM((n_all, 1, LANES), jnp.float32),
                 pltpu.SemaphoreType.DMA((turns, 4)),
                 pltpu.SemaphoreType.DMA((2,)),
-                pltpu.SemaphoreType.DMA((2, n_src)),
-                pltpu.SemaphoreType.DMA((2, n_src)),
-                pltpu.SemaphoreType.DMA((n_all,)),
-                pltpu.SemaphoreType.DMA((n_all,)),
+                pltpu.SemaphoreType.DMA,
+                pltpu.SemaphoreType.DMA,
+                pltpu.SemaphoreType.DMA,
+                pltpu.SemaphoreType.DMA,
             ],
             compiler_params=pltpu.CompilerParams(collective_id=0, has_side_effects=True),
             name="calibrate",
@@ -349,16 +315,17 @@
             weight.reshape(1, slots),
             damping.reshape(1, own),
         )
+        result = pltpu.with_memory_space_constraint(result, pltpu.VMEM)
         x, misfit = pl.pallas_call(
             hand_on,
             out_shape=(
                 jax.ShapeDtypeStruct((own, WIDTH), jnp.float32),
                 jax.ShapeDtypeStruct((1, 1), jnp.float32),
             ),
-            in_specs=[vmem, vmem],
+            in_specs=[vmem],
             out_specs=(vmem, vmem),
             name="hand_on",
-        )(x, misfit)
+        )(result)
         return x.T, misfit.reshape(())
 
     both = ("tm", "src")

time: 22.1 us -> 18.9 us (0.86)
  Pallas kernels: 20.6 us -> 17.5 us
    pallas_call x1, Pallas kernels: 18.7 us -> 16.9 us  [on_device(): pl.pallas_call(functools.partial(kernel, n_tm, n_src, chunk), out_shape=p...]
    pallas_call x1, Pallas kernels: 1.9 us -> 0.6 us  [on_device(): pl.pallas_call(hand_on, out_shape=(jax.ShapeDtypeStruct((own, WIDTH), jnp...]
where the time goes in v1:
time: 18.9 us; the launch traced here: 18.8 us
  Pallas kernels  17.5 us (93%)
  between operations  1.29 us (7%)
    pallas_call x1, Pallas kernels, on_device(): pl.pallas_call(functools.partial(kernel, n_tm, n_src, chunk), out_shape=p...  16.9 us
    pallas_call x1, Pallas kernels, on_device(): pl.pallas_call(hand_on, out_shape=(jax.ShapeDtypeStruct((own, WIDTH), jnp...  0.6 us

profile of v1, /device:TPU:0, one launch (start us, length us, event | category | flops | bytes accessed | tf_op | source)
XLA Modules:
  0.0 18.8 jit_solution(7896464243279061697)
XLA Ops:
  1.3 16.9 %calibrate.1.both_ref = f32[8,128]{1,0:T(8,128)S(1)} custom-call(s32[1]{0:T(128)S(6)} %copy.8.count_hbm, f32[16,16384]{1,0:T(8,128)} %design_hbm.1, s32[1,16384]{1,0:T(1,128)} %bitcast.6, f32[1,16384]{1,0:T(1,128)} %bitcast.7, f32[1,16384]{1,0:T(1,128)} %bitcast.8, f32[1,8]{1,0:T(1,128)} %bitcast.9), custom_call_target="tpu_custom_call" | custom-call | tf_op jit(solution)/shard_map/calibrate/pallas_call | solution.py:281
  18.2 0.6 %hand_on.1 = (f32[8,16]{1,0:T(8,128)}, f32[1,1]{1,0:T(1,128)}) custom-call(f32[8,128]{1,0:T(8,128)S(1)} %calibrate.1.both_ref), custom_call_target="tpu_custom_call" | custom-call | tf_op jit(solution)/shard_map/hand_on/pallas_call | solution.py:319

commit v2 on v1

--- a/solution.py
+++ b/solution.py
@@ -12,6 +12,7 @@
 PAIRS = WIDTH * (WIDTH + 1) // 2
 ROWS = PAIRS + WIDTH
 LANES = 128
+TILE = 256
 FOLD = 4
 
 
@@ -72,6 +73,13 @@
     return x, forward
 
 
+def ranked(k, me, n):
+    up = me >= n // 2
+    mine = jnp.where(up, me, n - 1 - me)
+    k = k + jnp.where(k >= mine, 1, 0)
+    return jnp.where(up, k, n - 1 - k)
+
+
 def far_first(n):
     q = max(n // 4, 1)
     order = []
@@ -79,6 +87,14 @@
         order += [3 * q + i, q + i]
     order += list(range(2 * q, 3 * q)) + list(range(1, q))
     return [p for p in dict.fromkeys(order) if 0 < p < n]
+
+
+def repeat(n, body, start):
+    if n <= 32:
+        for k in range(n):
+            start = body(k, start)
+        return start
+    return lax.fori_loop(0, n, body, start)
 
 
 def each(pairs, body, start):
@@ -92,12 +108,125 @@
     )
 
 
+def add_slots(accs, refs, begin, chunk, first_unit, count, weights):
+    design_ref, unit_ref, resid_ref, weight_ref = refs
+    chi, total = weights
+    for t in range(chunk // TILE):
+        cols = pl.ds(begin + t * TILE, TILE)
+        w = weight_ref[:, cols]
+        live = begin + t * TILE + lax.broadcasted_iota(jnp.int32, w.shape, 1) < count
+        w = jnp.where(live, w, 0.0)
+        r = resid_ref[:, cols]
+        wr = w * r
+        rows = stacked_rows(design_ref[0:HALF, cols], design_ref[HALF:WIDTH, cols], w, wr)
+        x = jnp.concatenate(rows, axis=0)
+        high = x.astype(jnp.bfloat16)
+        low = (x - high.astype(jnp.float32)).astype(jnp.bfloat16)
+        lhs = jnp.concatenate([high, low], axis=0)
+        unit = unit_ref[:, cols] - first_unit
+        wrr = wr * r
+        for k in range(TILE // LANES):
+            chi = chi + wrr[:, k * LANES:(k + 1) * LANES]
+            total = total + w[:, k * LANES:(k + 1) * LANES]
+        q = t % 2
+        for n, acc in enumerate(accs[q]):
+            pltpu.matmul_push_rhs(
+                one_hot(unit, n), staging_register=0, mxu_index=q, transpose=True
+            )
+            pltpu.matmul_acc_lhs(acc, lhs, load_staged_rhs=0)
+    return chi, total
+
+
+def one_hot(unit, n):
+    here = lax.broadcasted_iota(jnp.int32, (TILE, unit.shape[1]), 0) + n * TILE == unit
+    return jnp.where(here, 1.0, 0.0).astype(jnp.bfloat16)
+
+
+def clear(accs):
+    for q in range(2):
+        for acc in accs[q]:
+            pltpu.matmul_pop(acc)
+
+
+def drained(accs, units):
+    tiles = []
+    for n in range(len(accs[0])):
+        both = pltpu.matmul_pop(accs[0][n]) + pltpu.matmul_pop(accs[1][n])
+        tiles.append(both[0:ROWS] + both[ROWS:2 * ROWS])
+    return jnp.concatenate(tiles, axis=1)[:, 0:units]
+
+
+def with_sums(body, units):
+    tiles = -(-units // TILE)
+    shape = (2 * ROWS, TILE)
+    pl.run_scoped(
+        lambda *accs: body((accs[0:tiles], accs[tiles:2 * tiles])),
+        *[pltpu.ACC(q)(shape, jnp.float32) for q in range(2) for _ in range(tiles)],
+    )
+
+
+def beyond(
+    start, chunk,
+    count_ref, design_hbm, unit_hbm, resid_hbm, weight_hbm,
+    sums_ref, weights_ref,
+    design_ref, unit_ref, resid_ref, weight_ref, load,
+):
+    units = sums_ref.shape[1]
+    slots = design_hbm.shape[1]
+    first_unit = lax.axis_index("tm") * units
+    count = count_ref[0]
+    turns = (jnp.clip(count, start, slots) - start + chunk - 1) // chunk
+    arrays = (
+        (design_hbm, design_ref), (unit_hbm, unit_ref),
+        (resid_hbm, resid_ref), (weight_hbm, weight_ref),
+    )
+
+    def fetch(step, which):
+        far, here = arrays[which]
+        size = pl.ds(pl.multiple_of(start + step * chunk, LANES), chunk)
+        to = pl.ds(pl.multiple_of(step * chunk, LANES), chunk)
+        return pltpu.make_async_copy(far.at[:, size], here.at[:, to], load.at[step, which])
+
+    def fetch_all(step, c):
+        for which in range(4):
+            fetch(step, which).start()
+        return c
+
+    lax.fori_loop(0, turns, fetch_all, 0)
+
+    def body(accs):
+        zero = jnp.zeros((1, LANES), jnp.float32)
+
+        def add(step, weights):
+            for which in range(4):
+                fetch(step, which).wait()
+            return add_slots(
+                accs, (design_ref, unit_ref, resid_ref, weight_ref),
+                pl.multiple_of(step * chunk, LANES), chunk, first_unit, count - start, weights,
+            )
+
+        @pl.when(turns > 0)
+        def _():
+            clear(accs)
+            chi, total = lax.fori_loop(0, turns, add, (zero, zero))
+            sums_ref[...] = drained(accs, units)
+            weights_ref[:, 0:LANES] = chi
+            weights_ref[:, LANES:2 * LANES] = total
+
+        @pl.when(turns == 0)
+        def _():
+            sums_ref[...] = jnp.zeros_like(sums_ref)
+            weights_ref[...] = jnp.zeros_like(weights_ref)
+
+    with_sums(body, units)
+
+
 def kernel(
-    n_tm, n_src, chunk,
-    count_hbm, design_hbm, unit_hbm, resid_hbm, weight_hbm, damp_hbm,
+    n_tm, n_src, pieces,
+    count_hbm, design_hbm, unit_hbm, resid_hbm, weight_hbm, damp_hbm, beyond_ref, weights_ref,
     out_ref,
     count_ref, design_ref, unit_ref, resid_ref, weight_ref, damp_ref,
-    acc, extra, part, got, summed, spread, mine, heard,
+    sums_ref, kept_ref, extra, part, got, summed, spread, mine, heard,
     load, small, send_a, recv_a, send_b, recv_b,
 ):
     tm, src = lax.axis_index("tm"), lax.axis_index("src")
@@ -105,8 +234,7 @@
     me = tm * n_src + src
     own = damp_ref.shape[1]
     units = own * n_src
-    slots = design_ref.shape[1]
-    turns = slots // chunk
+    starts = [sum(pieces[:i]) for i in range(len(pieces))]
     order = far_first(n_src)
     near = [(0, p) for p in order]
     everyone = [(dt, p) for dt in range(n_tm - 1, 0, -1) for p in order + [0]] + near
@@ -118,15 +246,13 @@
 
     def fetch(step, which):
         far, here = arrays[which]
-        cols = pl.ds(pl.multiple_of(step * chunk, chunk), chunk)
+        cols = pl.ds(starts[step], pieces[step])
         return pltpu.make_async_copy(far.at[:, cols], here.at[:, cols], load.at[step, which])
 
     count_copy = pltpu.make_async_copy(count_hbm, count_ref, small.at[0])
     damp_copy = pltpu.make_async_copy(damp_hbm, damp_ref, small.at[1])
     count_copy.start()
-    for which in range(4):
-        fetch(0, which).start()
-    for step in range(1, turns):
+    for step in range(len(pieces)):
         for which in range(4):
             fetch(step, which).start()
     damp_copy.start()
@@ -145,41 +271,25 @@
     each(everyone, greet, 0)
 
     first_unit = tm * units
-    zero = jnp.zeros((1, LANES), jnp.float32)
     count_copy.wait()
     count = count_ref[0]
 
-    def accumulate(step, carry):
-        chi, total = carry
-        for which in range(4):
-            fetch(step, which).wait()
-        begin = pl.multiple_of(step * chunk, chunk)
-        cols = pl.ds(begin, chunk)
-        w = weight_ref[:, cols]
-        live = begin + lax.broadcasted_iota(jnp.int32, w.shape, 1) < count
-        w = jnp.where(live, w, 0.0)
-        r = resid_ref[:, cols]
-        wr = w * r
-        rows = stacked_rows(design_ref[0:HALF, cols], design_ref[HALF:WIDTH, cols], w, wr)
-        x = jnp.concatenate(rows, axis=0)
-        high = x.astype(jnp.bfloat16).astype(jnp.float32)
-        lhs = jnp.concatenate([high, x - high], axis=0).astype(jnp.bfloat16)
-        unit = unit_ref[:, cols] - first_unit
-        hot = lax.broadcasted_iota(jnp.int32, (units, chunk), 0) == unit
-        hot = jnp.where(hot, 1.0, 0.0).astype(jnp.bfloat16)
-        acc[...] += lax.dot_general(
-            lhs, hot, (((1,), (1,)), ((), ())), preferred_element_type=jnp.float32
-        )
-        wrr = wr * r
-        for t in range(chunk // LANES):
-            chi = chi + wrr[:, t * LANES:(t + 1) * LANES]
-            total = total + w[:, t * LANES:(t + 1) * LANES]
-        return chi, total
-
-    acc[...] = jnp.zeros_like(acc)
-    chi, total = lax.fori_loop(0, turns, accumulate, (zero, zero))
-
-    sums = acc[0:ROWS] + acc[ROWS:2 * ROWS]
+    def body(accs):
+        clear(accs)
+        weights = weights_ref[:, 0:LANES], weights_ref[:, LANES:2 * LANES]
+        for step in range(len(pieces)):
+            for which in range(4):
+                fetch(step, which).wait()
+            weights = add_slots(
+                accs, (design_ref, unit_ref, resid_ref, weight_ref),
+                starts[step], pieces[step], first_unit, count, weights,
+            )
+        sums_ref[...] = beyond_ref[...] + drained(accs, units)
+        kept_ref[:, 0:LANES], kept_ref[:, LANES:2 * LANES] = weights
+
+    with_sums(body, units)
+    sums = sums_ref[...]
+    chi, total = kept_ref[:, 0:LANES], kept_ref[:, LANES:2 * LANES]
     left = jnp.concatenate(
         [sums[LANES:ROWS], jnp.zeros((2 * LANES - ROWS, units), jnp.float32)], axis=0
     )
@@ -194,15 +304,15 @@
 
     pl.semaphore_wait(barrier, n_all - 1)
 
-    def send_one(dt, dp, c):
-        to = (src + dp) % n_src
+    def send_one(k, c):
+        to = ranked(k, src, n_src)
         pltpu.make_async_remote_copy(
             src_ref=part.at[to], dst_ref=got.at[src], send_sem=send_a, recv_sem=recv_a,
             device_id={"tm": tm, "src": to}, device_id_type=pl.DeviceIdType.MESH,
         ).start()
         return c
 
-    each(near, send_one, 0)
+    repeat(n_src - 1, send_one, 0)
     got[src] = part[src]
     others = got.at[pl.ds(0, n_src - 1)]
     pltpu.make_async_copy(others, others, recv_a).wait()
@@ -274,23 +384,48 @@
         own = damping.shape[0]
         units = own * n_src
         slots = design.shape[1]
-        chunk = 8192 if slots % 8192 == 0 else LANES
-        turns = slots // chunk
+        half = slots // 2
+        piece = half // 4 if half % 2048 == 0 else half
+        pieces = (piece, half - piece) if half > piece else (half,)
+        chunk = next(c for c in (4096, 2048, 1024, 512, 256) if (slots - half) % c == 0)
         anywhere = pl.BlockSpec(memory_space=pl.ANY)
         vmem = pl.BlockSpec(memory_space=pltpu.VMEM)
+        kept = lambda v: pltpu.with_memory_space_constraint(v, pltpu.VMEM)
+        unit_index, residual, weight = (
+            v.reshape(1, slots) for v in (unit_index, residual, weight)
+        )
+        rest = slots - half
+        sums, weights = pl.pallas_call(
+            functools.partial(beyond, half, chunk),
+            out_shape=(
+                pltpu.VMEM((ROWS, units), jnp.float32),
+                pltpu.VMEM((1, 2 * LANES), jnp.float32),
+            ),
+            in_specs=[pl.BlockSpec(memory_space=pltpu.SMEM)] + [anywhere] * 4,
+            out_specs=(vmem, vmem),
+            scratch_shapes=[
+                pltpu.VMEM((WIDTH, rest), jnp.float32),
+                pltpu.VMEM((1, rest), jnp.int32),
+                pltpu.VMEM((1, rest), jnp.float32),
+                pltpu.VMEM((1, rest), jnp.float32),
+                pltpu.SemaphoreType.DMA((rest // chunk, 4)),
+            ],
+            name="beyond",
+        )(obs_count, design, unit_index, residual, weight)
         result = pl.pallas_call(
-            functools.partial(kernel, n_tm, n_src, chunk),
+            functools.partial(kernel, n_tm, n_src, pieces),
             out_shape=pltpu.VMEM((own, LANES), jnp.float32),
-            in_specs=[anywhere] * 6,
+            in_specs=[anywhere] * 6 + [vmem] * 2,
             out_specs=vmem,
             scratch_shapes=[
                 pltpu.SMEM((1,), jnp.int32),
-                pltpu.VMEM((WIDTH, slots), jnp.float32),
-                pltpu.VMEM((1, slots), jnp.int32),
-                pltpu.VMEM((1, slots), jnp.float32),
-                pltpu.VMEM((1, slots), jnp.float32),
+                pltpu.VMEM((WIDTH, half), jnp.float32),
+                pltpu.VMEM((1, half), jnp.int32),
+                pltpu.VMEM((1, half), jnp.float32),
+                pltpu.VMEM((1, half), jnp.float32),
                 pltpu.VMEM((1, own), jnp.float32),
-                pltpu.VMEM((2 * ROWS, units), jnp.float32),
+                pltpu.VMEM((ROWS, units), jnp.float32),
+                pltpu.VMEM((1, 2 * LANES), jnp.float32),
                 pltpu.VMEM((units, LANES), jnp.float32),
                 pltpu.VMEM((n_src, own + own // FOLD, LANES), jnp.float32),
                 pltpu.VMEM((n_src, own + own // FOLD, LANES), jnp.float32),
@@ -298,7 +433,7 @@
                 pltpu.VMEM((own, LANES), jnp.float32),
                 pltpu.VMEM((1, LANES), jnp.float32),
                 pltpu.VMEM((n_all, 1, LANES), jnp.float32),
-                pltpu.SemaphoreType.DMA((turns, 4)),
+                pltpu.SemaphoreType.DMA((len(pieces), 4)),
                 pltpu.SemaphoreType.DMA((2,)),
                 pltpu.SemaphoreType.DMA,
                 pltpu.SemaphoreType.DMA,
@@ -310,12 +445,14 @@
         )(
             obs_count,
             design,
-            unit_index.reshape(1, slots),
-            residual.reshape(1, slots),
-            weight.reshape(1, slots),
+            unit_index,
+            residual,
+            weight,
             damping.reshape(1, own),
+            kept(sums),
+            kept(weights),
         )
-        result = pltpu.with_memory_space_constraint(result, pltpu.VMEM)
+        result = kept(result)
         x, misfit = pl.pallas_call(
             hand_on,
             out_shape=(

time: 18.9 us -> 18.4 us (0.974)
  Pallas kernels: 17.5 us -> 17 us
    pallas_call x1 -> x2, Pallas kernels: 16.9 us -> 16.4 us  [the longest x1 13.3 us: on_device(): pl.pallas_call(functools.partial(kernel, n_tm, n_src, pieces), out_shape=...]
where the time goes in v2:
time: 18.4 us; the launch traced here: 18.3 us
  Pallas kernels  17 us (92%)
  between operations  1.29 us (7%)
    pallas_call x1, Pallas kernels, on_device(): pl.pallas_call(functools.partial(kernel, n_tm, n_src, pieces), out_shape=...  13.3 us
    pallas_call x1, Pallas kernels, on_device(): pl.pallas_call(functools.partial(beyond, half, chunk), out_shape=(pltpu.V...  3.11 us
    pallas_call x1, Pallas kernels, on_device(): pl.pallas_call(hand_on, out_shape=(jax.ShapeDtypeStruct((own, WIDTH), jnp...  0.6 us

profile of v2, /device:TPU:0, one launch (start us, length us, event | category | flops | bytes accessed | tf_op | source)
XLA Modules:
  0.0 18.3 jit_solution(3272777826922849180)
XLA Ops:
  1.3 3.1 %beyond.1 = (f32[152,128]{1,0:T(8,128)S(1)}, f32[1,256]{1,0:T(1,128)S(1)}) custom-call(s32[1]{0:T(128)S(6)} %copy.8.count_ref.count_hbm, f32[16,16384]{1,0:T(8,128)} %design_hbm.3, s32[1,16384]{1,0:T(1,128)} %bitcast.6, f32[1,16384]{1,0:T(1,128)} %bitcast.8, f32[1,16384]{1,0:T(1,128)} %bitcast.10), custom_call_target="tpu_custom_call" | custom-call | tf_op jit(solution)/shard_map/beyond/pallas_call | solution.py:398
  4.4 13.3 %calibrate.1.both_ref = f32[8,128]{1,0:T(8,128)S(1)} custom-call(s32[1]{0:T(128)S(6)} %copy.8.count_ref.count_hbm, f32[16,16384]{1,0:T(8,128)} %design_hbm.3, s32[1,16384]{1,0:T(1,128)} %bitcast.7, f32[1,16384]{1,0:T(1,128)} %bitcast.9, f32[1,16384]{1,0:T(1,128)} %bitcast.11, f32[1,8]{1,0:T(1,128)} %bitcast.12, f32[152,128]{1,0:T(8,128)S(1)} %get-tuple-element.6.beyond_ref, ...), custom_call_target="tpu_custom_call" | custom-call | tf_op jit(solution)/shard_map/calibrate/pallas_call | solution.py:415
  17.7 0.6 %hand_on.1 = (f32[8,16]{1,0:T(8,128)}, f32[1,1]{1,0:T(1,128)}) custom-call(f32[8,128]{1,0:T(8,128)S(1)} %calibrate.1.both_ref), custom_call_target="tpu_custom_call" | custom-call | tf_op jit(solution)/shard_map/hand_on/pallas_call | solution.py:456

commit v3 on v2

v3 whole, which is shorter than its diff:
```python
import functools

import jax
import jax.numpy as jnp
from jax import lax
from jax.experimental import pallas as pl
from jax.experimental.pallas import tpu as pltpu
from jax.sharding import PartitionSpec as P

WIDTH = 16
HALF = 8
PAIRS = WIDTH * (WIDTH + 1) // 2
ROWS = PAIRS + WIDTH
EVEN = ROWS // WIDTH * WIDTH
LANES = 128
TILE = 256
FOLD = 4


def pair_row(i, j):
    k = (j - i) % WIDTH
    if k > HALF or (k == HALF and i >= HALF):
        i, j = j, i
        k = (j - i) % WIDTH
    return k * WIDTH + i


def stacked_rows(d0, d1, w, wr):
    w0, w1 = d0 * w, d1 * w
    rows = [d0 * w0, d1 * w1]
    sub = lax.broadcasted_iota(jnp.int32, d0.shape, 0)
    for k in range(1, HALF):
        r0 = pltpu.roll(w0, HALF - k, 0)
        r1 = pltpu.roll(w1, HALF - k, 0)
        low = sub < HALF - k
        rows.append(d0 * jnp.where(low, r0, r1))
        rows.append(d1 * jnp.where(low, r1, r0))
    rows.append(d0 * w1)
    rows.append(d0 * wr)
    rows.append(d1 * wr)
    return rows


def rsqrt(value):
    guess = lax.rsqrt(value)
    return guess * (1.5 - 0.5 * value * guess * guess)


def solve(entry, rhs, damping):
    a = {}
    for i in range(WIDTH):
        for j in range(i + 1):
            a[i, j] = entry(i, j)
        a[i, i] = a[i, i] + damping
    b = [rhs(i) for i in range(WIDTH)]
    inverse, forward = [], []
    for j in range(WIDTH):
        inv = rsqrt(a[j, j])
        inverse.append(inv)
        for i in range(j + 1, WIDTH):
            a[i, j] = a[i, j] * inv
        y = b[j] * inv
        forward.append(y)
        for i in range(j + 1, WIDTH):
            b[i] = b[i] - a[i, j] * y
            for k in range(j + 1, i + 1):
                a[i, k] = a[i, k] - a[i, j] * a[k, j]
    run = list(forward)
    x = [None] * WIDTH
    for i in reversed(range(WIDTH)):
        x[i] = run[i] * inverse[i]
        for k in range(i):
            run[k] = run[k] - a[i, k] * x[i]
    return x, forward


def skipping(k, me):
    return k + jnp.where(k >= me, 1, 0)


def ranked(k, me, n, up):
    k = skipping(k, jnp.where(up, me, n - 1 - me))
    return jnp.where(up, k, n - 1 - k)


def repeat(n, body):
    if n <= 32:
        for k in range(n):
            body(k)
    elif n:
        lax.fori_loop(0, n, lambda k, c: (body(k), c)[1], 0)


def solved_by(n_src):
    q = n_src // 4
    return [(w, w - q if w < 2 * q else w + q) for w in range(q, n_src - q)]


def add_slots(accs, refs, begin, chunk, first_unit, units, count, weights):
    design_ref, unit_ref, resid_ref, weight_ref = refs
    chi, total = weights
    for t in range(chunk // TILE):
        cols = pl.ds(begin + t * TILE, TILE)
        w = weight_ref[:, cols]
        live = begin + t * TILE + lax.broadcasted_iota(jnp.int32, w.shape, 1) < count
        w = jnp.where(live, w, 0.0)
        r = resid_ref[:, cols]
        wr = w * r
        rows = stacked_rows(design_ref[0:HALF, cols], design_ref[HALF:WIDTH, cols], w, wr)
        x = jnp.concatenate(rows, axis=0)
        high = x.astype(jnp.bfloat16).astype(jnp.float32)
        low = x - high
        lhs = jnp.concatenate(
            [high[0:EVEN], low[0:EVEN], high[EVEN:ROWS], low[EVEN:ROWS]], axis=0
        ).astype(jnp.bfloat16)
        unit = unit_ref[:, cols] - first_unit
        wrr = wr * r
        for k in range(TILE // LANES):
            chi = chi + wrr[:, k * LANES:(k + 1) * LANES]
            total = total + w[:, k * LANES:(k + 1) * LANES]
        q = t % 2
        for n, acc in enumerate(accs[q]):
            pltpu.matmul_push_rhs(
                one_hot(unit, n, units), staging_register=0, mxu_index=q, transpose=True
            )
            pltpu.matmul_acc_lhs(acc, lhs, load_staged_rhs=0)
    return chi, total


def one_hot(unit, n, units):
    rows = min(units - n * TILE, TILE)
    here = lax.broadcasted_iota(jnp.int16, (rows, TILE), 0) == (unit - n * TILE).astype(jnp.int16)
    hot = jnp.where(here, jnp.bfloat16(1), jnp.bfloat16(0))
    if rows < TILE:
        hot = jnp.concatenate([hot, jnp.zeros((TILE - rows, TILE), jnp.bfloat16)], axis=0)
    return hot


def clear(accs):
    for q in range(2):
        for acc in accs[q]:
            pltpu.matmul_pop(acc)


def drained(accs, units):
    tiles = []
    for n in range(len(accs[0])):
        both = pltpu.matmul_pop(accs[0][n]) + pltpu.matmul_pop(accs[1][n])
        tiles.append(jnp.concatenate(
            [both[0:EVEN] + both[EVEN:2 * EVEN], both[2 * EVEN:EVEN + ROWS] + both[EVEN + ROWS:]],
            axis=0,
        ))
    return jnp.concatenate(tiles, axis=1)[:, 0:units]


def with_sums(body, units):
    tiles = -(-units // TILE)
    shape = (2 * ROWS, TILE)
    pl.run_scoped(
        lambda *accs: body((accs[0:tiles], accs[tiles:2 * tiles])),
        *[pltpu.ACC(q)(shape, jnp.float32) for q in range(2) for _ in range(tiles)],
    )


def beyond(
    start, chunk,
    count_ref, design_hbm, unit_hbm, resid_hbm, weight_hbm,
    sums_ref, weights_ref,
    design_ref, unit_ref, resid_ref, weight_ref, load,
):
    units = sums_ref.shape[1]
    slots = design_hbm.shape[1]
    first_unit = lax.axis_index("tm") * units
    count = count_ref[0]
    turns = (jnp.clip(count, start, slots) - start + chunk - 1) // chunk
    arrays = (
        (design_hbm, design_ref), (unit_hbm, unit_ref),
        (resid_hbm, resid_ref), (weight_hbm, weight_ref),
    )

    def fetch(step, which):
        far, here = arrays[which]
        size = pl.ds(pl.multiple_of(start + step * chunk, LANES), chunk)
        to = pl.ds(pl.multiple_of(step * chunk, LANES), chunk)
        return pltpu.make_async_copy(far.at[:, size], here.at[:, to], load.at[step, which])

    def fetch_all(step, c):
        for which in range(4):
            fetch(step, which).start()
        return c

    lax.fori_loop(0, turns, fetch_all, 0)

    def body(accs):
        zero = jnp.zeros((1, LANES), jnp.float32)

        def add(step, weights):
            for which in range(4):
                fetch(step, which).wait()
            return add_slots(
                accs, (design_ref, unit_ref, resid_ref, weight_ref),
                pl.multiple_of(step * chunk, LANES), chunk, first_unit, units, count - start, weights,
            )

        @pl.when(turns > 0)
        def _():
            clear(accs)
            chi, total = lax.fori_loop(0, turns, add, (zero, zero))
            sums_ref[...] = drained(accs, units)
            weights_ref[:, 0:LANES] = chi
            weights_ref[:, LANES:2 * LANES] = total

        @pl.when(turns == 0)
        def _():
            sums_ref[...] = jnp.zeros_like(sums_ref)
            weights_ref[...] = jnp.zeros_like(weights_ref)

    with_sums(body, units)


def kernel(
    n_tm, n_src, pieces,
    count_ref, design_hbm, unit_hbm, resid_hbm, weight_hbm, damp_hbm, beyond_ref, weights_ref,
    out_ref,
    design_ref, unit_ref, resid_ref, weight_ref, damp_ref,
    sums_ref, kept_ref, extra, part, got, summed, spread, mine, heard, x_away, x_here,
    load, small, send_a, recv_a, send_b, recv_b, send_c, recv_c,
):
    tm, src = lax.axis_index("tm"), lax.axis_index("src")
    own = damp_ref.shape[1]
    units = own * n_src
    pairs = solved_by(n_src)
    n_solve = len(pairs)
    first_solver = pairs[0][0]
    lanes = own * n_src // n_solve
    n_outer = n_src - n_solve
    solves = (src >= first_solver) & (src < first_solver + n_solve)
    rank = src - first_solver
    up = src >= n_src // 2
    starts = [sum(pieces[:i]) for i in range(len(pieces))]

    arrays = (
        (design_hbm, design_ref), (unit_hbm, unit_ref),
        (resid_hbm, resid_ref), (weight_hbm, weight_ref),
    )

    def fetch(step, which):
        far, here = arrays[which]
        cols = pl.ds(starts[step], pieces[step])
        return pltpu.make_async_copy(far.at[:, cols], here.at[:, cols], load.at[step, which])

    x_away[...] = jnp.zeros_like(x_away)
    damp_copy = pltpu.make_async_copy(damp_hbm, damp_ref, small)
    for step in range(len(pieces)):
        for which in range(4):
            fetch(step, which).start()
    damp_copy.start()

    barrier = pltpu.get_barrier_semaphore()

    def greet(t, p):
        pl.semaphore_signal(
            barrier, inc=1, device_id={"tm": t, "src": p}, device_id_type=pl.DeviceIdType.MESH
        )

    @pl.when(solves)
    def _():
        repeat(n_outer, lambda k: greet(tm, k + jnp.where(k >= first_solver, n_solve, 0)))
        repeat(n_solve - 1, lambda k: greet(tm, first_solver + skipping(k, rank)))

    @pl.when(jnp.logical_not(solves))
    def _():
        repeat(n_solve, lambda k: greet(tm, first_solver + k))

    for dt in range(1, n_tm):
        repeat(n_solve, lambda k: greet((tm + dt) % n_tm, first_solver + k))

    first_unit = tm * units
    count = count_ref[0]

    def body(accs):
        clear(accs)
        weights = weights_ref[:, 0:LANES], weights_ref[:, LANES:2 * LANES]
        for step in range(len(pieces)):
            for which in range(4):
                fetch(step, which).wait()
            weights = add_slots(
                accs, (design_ref, unit_ref, resid_ref, weight_ref),
                starts[step], pieces[step], first_unit, units, count, weights,
            )
        sums_ref[...] = beyond_ref[...] + drained(accs, units)
        kept_ref[:, 0:LANES], kept_ref[:, LANES:2 * LANES] = weights

    with_sums(body, units)
    sums = sums_ref[...]
    damp_copy.wait()
    damping = jnp.concatenate([damp_ref[...]] * n_src, axis=1)
    block = lax.broadcasted_iota(jnp.int32, damping.shape, 1) // own
    damping = jnp.where(block == src, damping, 0.0)
    fill = [jnp.zeros((1, units - LANES), jnp.float32)] if units > LANES else []
    chi = jnp.concatenate([kept_ref[:, 0:LANES]] + fill, axis=1)
    total = jnp.concatenate([kept_ref[:, LANES:2 * LANES]] + fill, axis=1)
    left = jnp.concatenate(
        [sums[LANES:ROWS], damping, chi, total,
         jnp.zeros((2 * LANES - ROWS - 3, units), jnp.float32)], axis=0
    )

    def by_solver(rows):
        return jnp.concatenate(
            [rows[b * own:(b + 1) * own] for pair in pairs for b in pair], axis=0
        )

    extra[...] = by_solver(jnp.transpose(left))
    part[:, 0:lanes, :] = by_solver(jnp.transpose(sums[0:LANES])).reshape(n_solve, lanes, LANES)
    packed = extra[pl.ds(0, units // FOLD, stride=FOLD), :]
    lane = lax.broadcasted_iota(jnp.int32, packed.shape, 1) // (LANES // FOLD)
    for b in range(1, FOLD):
        more = extra[pl.ds(b, units // FOLD, stride=FOLD), :]
        packed = jnp.where(lane == b, pltpu.roll(more, b * (LANES // FOLD), 1), packed)
    part[:, lanes:, :] = packed.reshape(n_solve, lanes // FOLD, LANES)

    def send_to(k):
        pltpu.make_async_remote_copy(
            src_ref=part.at[k], dst_ref=got.at[src], send_sem=send_a, recv_sem=recv_a,
            device_id={"tm": tm, "src": first_solver + k},
            device_id_type=pl.DeviceIdType.MESH,
        ).start()

    def wait_bytes(ref, n, sem):
        some = ref.at[pl.ds(0, n)]
        pltpu.make_async_copy(some, some, sem).wait()

    def hand_over(p):
        return pltpu.make_async_remote_copy(
            src_ref=x_away, dst_ref=x_here, send_sem=send_c, recv_sem=recv_c,
            device_id={"tm": tm, "src": p}, device_id_type=pl.DeviceIdType.MESH,
        )

    me = tm * n_solve + rank

    def tell(t, p):
        pltpu.make_async_remote_copy(
            src_ref=mine, dst_ref=heard.at[me], send_sem=send_b, recv_sem=recv_b,
            device_id={"tm": t, "src": p}, device_id_type=pl.DeviceIdType.MESH,
        ).start()

    def tell_both(k):
        p = skipping(k, src)
        for t in range(n_tm):
            tell(t, p)

    @pl.when(solves)
    def _():
        pl.semaphore_wait(barrier, n_tm * n_src - 1)
        repeat(n_solve - 1, lambda k: send_to(ranked(k, rank, n_solve, up)))
        got[src] = part[rank]
        wait_bytes(got, n_src - 1, recv_a)
        both = got[0]
        for p in range(1, n_src):
            both = both + got[p]
        whole, ends = both[0:lanes], both[lanes:]
        for a in range(lanes // FOLD):
            for b in range(FOLD):
                row = ends[a:a + 1]
                spread[pl.ds(a * FOLD + b, 1), :] = (
                    pltpu.roll(row, LANES - b * (LANES // FOLD), 1) if b else row
                )
        summed[0:LANES, :] = jnp.transpose(whole)
        summed[LANES:2 * LANES, :] = jnp.transpose(spread[...])
        damping, chi, total = (summed[pl.ds(ROWS + i, 1), :] for i in range(3))
        x, forward = solve(
            lambda i, j: summed[pl.ds(pair_row(i, j), 1), :],
            lambda i: summed[pl.ds(PAIRS + i, 1), :],
            damping,
        )
        terms = jnp.zeros_like(damping)
        squared = jnp.zeros_like(damping)
        for i in range(WIDTH):
            terms = terms + forward[i] * forward[i]
            squared = squared + x[i] * x[i]
        terms = terms + damping * squared
        none = jnp.zeros((1, LANES // 2 - lanes), jnp.float32)
        mine[...] = jnp.concatenate([chi - terms, none, total, none], axis=1)
        heard[me] = mine[...]
        repeat(n_src - 1, tell_both)
        for dt in range(1, n_tm):
            tell((tm + dt) % n_tm, src)
        answer = jnp.transpose(jnp.concatenate(x, axis=0))
        x_away[:, 0:WIDTH] = answer[own:]
        copy = hand_over(jnp.where(up, src + n_src // 4, src - n_src // 4))
        copy.start()
        out_ref[:, 0:WIDTH] = answer[0:own]
        wait_bytes(part, n_solve - 1, send_a)
        wait_bytes(heard, n_tm * n_solve - 1, recv_b)

    @pl.when(jnp.logical_not(solves))
    def _():
        pl.semaphore_wait(barrier, n_solve)
        repeat(n_solve, lambda k: send_to(jnp.where(up, k, n_solve - 1 - k)))
        hand_over(src).wait_recv()
        out_ref[...] = x_here[...]
        wait_bytes(part, n_solve, send_a)
        wait_bytes(heard, n_tm * n_solve, recv_b)

    both = jnp.sum(heard[...].reshape(n_tm * n_solve, LANES), axis=0, keepdims=True)
    front = lax.broadcasted_iota(jnp.int32, (1, LANES), 1) < LANES // 2
    chi_all = jnp.sum(jnp.where(front, both, 0.0), axis=1, keepdims=True)
    total_all = jnp.sum(jnp.where(front, 0.0, both), axis=1, keepdims=True)
    out_ref[0:1, WIDTH:WIDTH + 1] = chi_all / total_all

    @pl.when(solves)
    def _():
        hand_over(src).wait_send()
        rest = n_tm * n_src - 1
        while rest > 0:
            some = min(rest, n_tm * n_solve)
            wait_bytes(heard, some, send_b)
            rest -= some


def hand_on(both_ref, x_out, misfit_out):
    x_out[...] = both_ref[:, 0:WIDTH]
    misfit_out[...] = both_ref[0:1, WIDTH:WIDTH + 1]


def solution(mesh):
    n_tm, n_src = mesh.shape["tm"], mesh.shape["src"]

    def on_device(design, unit_index, residual, weight, obs_count, damping):
        own = damping.shape[0]
        units = own * n_src
        slots = design.shape[1]
        half = slots // 2
        piece = half // 4 if half % 2048 == 0 else half
        pieces = (piece, half - piece) if half > piece else (half,)
        chunk = next(c for c in (4096, 2048, 1024, 512, 256) if (slots - half) % c == 0)
        n_solve = len(solved_by(n_src))
        lanes = units // n_solve
        anywhere = pl.BlockSpec(memory_space=pl.ANY)
        vmem = pl.BlockSpec(memory_space=pltpu.VMEM)
        kept = lambda v: pltpu.with_memory_space_constraint(v, pltpu.VMEM)
        unit_index, residual, weight = (
            v.reshape(1, slots) for v in (unit_index, residual, weight)
        )
        rest = slots - half
        sums, weights = pl.pallas_call(
            functools.partial(beyond, half, chunk),
            out_shape=(
                pltpu.VMEM((ROWS, units), jnp.float32),
                pltpu.VMEM((1, 2 * LANES), jnp.float32),
            ),
            in_specs=[pl.BlockSpec(memory_space=pltpu.SMEM)] + [anywhere] * 4,
            out_specs=(vmem, vmem),
            scratch_shapes=[
                pltpu.VMEM((WIDTH, rest), jnp.float32),
                pltpu.VMEM((1, rest), jnp.int32),
                pltpu.VMEM((1, rest), jnp.float32),
                pltpu.VMEM((1, rest), jnp.float32),
                pltpu.SemaphoreType.DMA((rest // chunk, 4)),
            ],
            name="beyond",
        )(obs_count, design, unit_index, residual, weight)
        result = pl.pallas_call(
            functools.partial(kernel, n_tm, n_src, pieces),
            out_shape=pltpu.VMEM((own, LANES), jnp.float32),
            in_specs=[pl.BlockSpec(memory_space=pltpu.SMEM)] + [anywhere] * 5 + [vmem] * 2,
            out_specs=vmem,
            scratch_shapes=[
                pltpu.VMEM((WIDTH, half), jnp.float32),
                pltpu.VMEM((1, half), jnp.int32),
                pltpu.VMEM((1, half), jnp.float32),
                pltpu.VMEM((1, half), jnp.float32),
                pltpu.VMEM((1, own), jnp.float32),
                pltpu.VMEM((ROWS, units), jnp.float32),
                pltpu.VMEM((1, 2 * LANES), jnp.float32),
                pltpu.VMEM((units, LANES), jnp.float32),
                pltpu.VMEM((n_solve, lanes + lanes // FOLD, LANES), jnp.float32),
                pltpu.VMEM((n_src, lanes + lanes // FOLD, LANES), jnp.float32),
                pltpu.VMEM((2 * LANES, lanes), jnp.float32),
                pltpu.VMEM((lanes, LANES), jnp.float32),
                pltpu.VMEM((1, LANES), jnp.float32),
                pltpu.VMEM((n_tm * n_solve, 1, LANES), jnp.float32),
                pltpu.VMEM((own, LANES), jnp.float32),
                pltpu.VMEM((own, LANES), jnp.float32),
                pltpu.SemaphoreType.DMA((len(pieces), 4)),
            ] + [pltpu.SemaphoreType.DMA] * 7,
            compiler_params=pltpu.CompilerParams(collective_id=0, has_side_effects=True),
            name="calibrate",
        )(
            obs_count,
            design,
            unit_index,
            residual,
            weight,
            damping.reshape(1, own),
            kept(sums),
            kept(weights),
        )
        result = kept(result)
        x, misfit = pl.pallas_call(
            hand_on,
            out_shape=(
                jax.ShapeDtypeStruct((own, WIDTH), jnp.float32),
                jax.ShapeDtypeStruct((1, 1), jnp.float32),
            ),
            in_specs=[vmem],
            out_specs=(vmem, vmem),
            name="hand_on",
        )(result)
        return x.T, misfit.reshape(())

    both = ("tm", "src")
    return jax.shard_map(
        on_device,
        mesh=mesh,
        in_specs=(P(None, both), P(both), P(both), P(both), P(both), P(both)),
        out_specs=(P(None, both), P()),
        check_vma=False,
    )
```

time: 18.4 us -> 17.4 us (0.946)
  Pallas kernels: 17 us -> 15.9 us
    pallas_call x1, Pallas kernels: 13.3 us -> 12.5 us  [on_device(): pl.pallas_call(functools.partial(kernel, n_tm, n_src, pieces), out_shape=...]
    pallas_call x1, Pallas kernels: 3.11 us -> 2.86 us  [on_device(): pl.pallas_call(functools.partial(beyond, half, chunk), out_shape=(pltpu.V...]
where the time goes in v3:
time: 17.4 us; the launch traced here: 17.2 us
  Pallas kernels  15.9 us (91%)
  between operations  1.29 us (7%)
    pallas_call x1, Pallas kernels, on_device(): pl.pallas_call(functools.partial(kernel, n_tm, n_src, pieces), out_shape=...  12.5 us
    pallas_call x1, Pallas kernels, on_device(): pl.pallas_call(functools.partial(beyond, half, chunk), out_shape=(pltpu.V...  2.86 us
    pallas_call x1, Pallas kernels, on_device(): pl.pallas_call(hand_on, out_shape=(jax.ShapeDtypeStruct((own, WIDTH), jnp...  0.6 us

profile of v3, /device:TPU:0, one launch (start us, length us, event | category | flops | bytes accessed | tf_op | source)
XLA Modules:
  0.0 17.2 jit_solution(11366048529231249461)
XLA Ops:
  1.3 2.9 %beyond.1 = (f32[152,128]{1,0:T(8,128)S(1)}, f32[1,256]{1,0:T(1,128)S(1)}) custom-call(s32[1]{0:T(128)S(6)} %copy.8.count_ref, f32[16,16384]{1,0:T(8,128)} %design_hbm.3, s32[1,16384]{1,0:T(1,128)} %bitcast.6, f32[1,16384]{1,0:T(1,128)} %bitcast.8, f32[1,16384]{1,0:T(1,128)} %bitcast.10), custom_call_target="tpu_custom_call" | custom-call | tf_op jit(solution)/shard_map/beyond/pallas_call | solution.py:446
  4.1 12.5 %calibrate.1.both_ref = f32[8,128]{1,0:T(8,128)S(1)} custom-call(s32[1]{0:T(128)S(6)} %copy.8.count_ref, f32[16,16384]{1,0:T(8,128)} %design_hbm.3, s32[1,16384]{1,0:T(1,128)} %bitcast.7, f32[1,16384]{1,0:T(1,128)} %bitcast.9, f32[1,16384]{1,0:T(1,128)} %bitcast.11, f32[1,8]{1,0:T(1,128)} %bitcast.12, f32[152,128]{1,0:T(8,128)S(1)} %get-tuple-element.6.beyond_ref, ...), custom_call_target="tpu_custom_call" | custom-call | tf_op jit(solution)/shard_map/calibrate/pallas_call | solution.py:463
  16.6 0.6 %hand_on.1 = (f32[8,16]{1,0:T(8,128)}, f32[1,1]{1,0:T(1,128)}) custom-call(f32[8,128]{1,0:T(8,128)S(1)} %calibrate.1.both_ref), custom_call_target="tpu_custom_call" | custom-call | tf_op jit(solution)/shard_map/hand_on/pallas_call | solution.py:500

commit v4 on v3

--- a/solution.py
+++ b/solution.py
@@ -93,7 +93,11 @@
 
 def solved_by(n_src):
     q = n_src // 4
-    return [(w, w - q if w < 2 * q else w + q) for w in range(q, n_src - q)]
+    blocks = []
+    for w in range(q + 1, n_src - q, 2):
+        away = -q if w < 2 * q else q
+        blocks.append((w, w - 1, w + away, w - 1 + away))
+    return blocks
 
 
 def add_slots(accs, refs, begin, chunk, first_unit, units, count, weights):
@@ -229,13 +233,12 @@
     tm, src = lax.axis_index("tm"), lax.axis_index("src")
     own = damp_ref.shape[1]
     units = own * n_src
-    pairs = solved_by(n_src)
-    n_solve = len(pairs)
-    first_solver = pairs[0][0]
+    shares = solved_by(n_src)
+    n_solve = len(shares)
+    first_solver = shares[0][0]
     lanes = own * n_src // n_solve
-    n_outer = n_src - n_solve
-    solves = (src >= first_solver) & (src < first_solver + n_solve)
-    rank = src - first_solver
+    solves = (src >= first_solver) & (src < first_solver + 2 * n_solve) & (src % 2 == 1)
+    rank = (src - first_solver) // 2
     up = src >= n_src // 2
     starts = [sum(pieces[:i]) for i in range(len(pieces))]
 
@@ -265,15 +268,14 @@
 
     @pl.when(solves)
     def _():
-        repeat(n_outer, lambda k: greet(tm, k + jnp.where(k >= first_solver, n_solve, 0)))
-        repeat(n_solve - 1, lambda k: greet(tm, first_solver + skipping(k, rank)))
+        repeat(n_src - 1, lambda k: greet(tm, skipping(k, src)))
 
     @pl.when(jnp.logical_not(solves))
     def _():
-        repeat(n_solve, lambda k: greet(tm, first_solver + k))
+        repeat(n_solve, lambda k: greet(tm, first_solver + 2 * k))
 
     for dt in range(1, n_tm):
-        repeat(n_solve, lambda k: greet((tm + dt) % n_tm, first_solver + k))
+        repeat(n_solve, lambda k: greet((tm + dt) % n_tm, first_solver + 2 * k))
 
     first_unit = tm * units
     count = count_ref[0]
@@ -307,7 +309,7 @@
 
     def by_solver(rows):
         return jnp.concatenate(
-            [rows[b * own:(b + 1) * own] for pair in pairs for b in pair], axis=0
+            [rows[b * own:(b + 1) * own] for share in shares for b in share], axis=0
         )
 
     extra[...] = by_solver(jnp.transpose(left))
@@ -322,7 +324,7 @@
     def send_to(k):
         pltpu.make_async_remote_copy(
             src_ref=part.at[k], dst_ref=got.at[src], send_sem=send_a, recv_sem=recv_a,
-            device_id={"tm": tm, "src": first_solver + k},
+            device_id={"tm": tm, "src": first_solver + 2 * k},
             device_id_type=pl.DeviceIdType.MESH,
         ).start()
 
@@ -330,9 +332,12 @@
         some = ref.at[pl.ds(0, n)]
         pltpu.make_async_copy(some, some, sem).wait()
 
-    def hand_over(p):
+    away = jnp.where(up, n_src // 4, -(n_src // 4))
+
+    def hand_over(i, p):
         return pltpu.make_async_remote_copy(
-            src_ref=x_away, dst_ref=x_here, send_sem=send_c, recv_sem=recv_c,
+            src_ref=x_away.at[pl.ds(i * own, own)], dst_ref=x_here,
+            send_sem=send_c, recv_sem=recv_c,
             device_id={"tm": tm, "src": p}, device_id_type=pl.DeviceIdType.MESH,
         )
 
@@ -386,9 +391,9 @@
         for dt in range(1, n_tm):
             tell((tm + dt) % n_tm, src)
         answer = jnp.transpose(jnp.concatenate(x, axis=0))
-        x_away[:, 0:WIDTH] = answer[own:]
-        copy = hand_over(jnp.where(up, src + n_src // 4, src - n_src // 4))
-        copy.start()
+        x_away[:, 0:WIDTH] = answer
+        for i, p in ((2, src + away), (3, src - 1 + away), (1, src - 1)):
+            hand_over(i, p).start()
         out_ref[:, 0:WIDTH] = answer[0:own]
         wait_bytes(part, n_solve - 1, send_a)
         wait_bytes(heard, n_tm * n_solve - 1, recv_b)
@@ -397,7 +402,7 @@
     def _():
         pl.semaphore_wait(barrier, n_solve)
         repeat(n_solve, lambda k: send_to(jnp.where(up, k, n_solve - 1 - k)))
-        hand_over(src).wait_recv()
+        hand_over(0, src).wait_recv()
         out_ref[...] = x_here[...]
         wait_bytes(part, n_solve, send_a)
         wait_bytes(heard, n_tm * n_solve, recv_b)
@@ -410,7 +415,8 @@
 
     @pl.when(solves)
     def _():
-        hand_over(src).wait_send()
+        some = x_away.at[pl.ds(own, 3 * own)]
+        pltpu.make_async_copy(some, some, send_c).wait()
         rest = n_tm * n_src - 1
         while rest > 0:
             some = min(rest, n_tm * n_solve)
@@ -480,7 +486,7 @@
                 pltpu.VMEM((lanes, LANES), jnp.float32),
                 pltpu.VMEM((1, LANES), jnp.float32),
                 pltpu.VMEM((n_tm * n_solve, 1, LANES), jnp.float32),
-                pltpu.VMEM((own, LANES), jnp.float32),
+                pltpu.VMEM((lanes, LANES), jnp.float32),
                 pltpu.VMEM((own, LANES), jnp.float32),
                 pltpu.SemaphoreType.DMA((len(pieces), 4)),
             ] + [pltpu.SemaphoreType.DMA] * 7,

time: 17.4 us -> 16.6 us (0.954)
  Pallas kernels: 15.9 us -> 15.2 us
    pallas_call x1, Pallas kernels: 12.5 us -> 11.7 us  [on_device(): pl.pallas_call(functools.partial(kernel, n_tm, n_src, pieces), out_shape=...]
where the time goes in v4:
time: 16.6 us; the launch traced here: 16.5 us
  Pallas kernels  15.2 us (92%)
  between operations  1.29 us (8%)
    pallas_call x1, Pallas kernels, on_device(): pl.pallas_call(functools.partial(kernel, n_tm, n_src, pieces), out_shape=...  11.7 us
    pallas_call x1, Pallas kernels, on_device(): pl.pallas_call(functools.partial(beyond, half, chunk), out_shape=(pltpu.V...  2.86 us
    pallas_call x1, Pallas kernels, on_device(): pl.pallas_call(hand_on, out_shape=(jax.ShapeDtypeStruct((own, WIDTH), jnp...  0.6 us

profile of v4, /device:TPU:0, one launch (start us, length us, event | category | flops | bytes accessed | tf_op | source)
XLA Modules:
  0.0 16.5 jit_solution(5871821618880833336)
XLA Ops:
  1.3 2.9 %beyond.1 = (f32[152,128]{1,0:T(8,128)S(1)}, f32[1,256]{1,0:T(1,128)S(1)}) custom-call(s32[1]{0:T(128)S(6)} %copy.8.count_ref, f32[16,16384]{1,0:T(8,128)} %design_hbm.3, s32[1,16384]{1,0:T(1,128)} %bitcast.6, f32[1,16384]{1,0:T(1,128)} %bitcast.8, f32[1,16384]{1,0:T(1,128)} %bitcast.10), custom_call_target="tpu_custom_call" | custom-call | tf_op jit(solution)/shard_map/beyond/pallas_call | solution.py:452
  4.1 11.7 %calibrate.1.both_ref = f32[8,128]{1,0:T(8,128)S(1)} custom-call(s32[1]{0:T(128)S(6)} %copy.8.count_ref, f32[16,16384]{1,0:T(8,128)} %design_hbm.3, s32[1,16384]{1,0:T(1,128)} %bitcast.7, f32[1,16384]{1,0:T(1,128)} %bitcast.9, f32[1,16384]{1,0:T(1,128)} %bitcast.11, f32[1,8]{1,0:T(1,128)} %bitcast.12, f32[152,128]{1,0:T(8,128)S(1)} %get-tuple-element.6.beyond_ref, ...), custom_call_target="tpu_custom_call" | custom-call | tf_op jit(solution)/shard_map/calibrate/pallas_call | solution.py:469
  15.9 0.6 %hand_on.1 = (f32[8,16]{1,0:T(8,128)}, f32[1,1]{1,0:T(1,128)}) custom-call(f32[8,128]{1,0:T(8,128)S(1)} %calibrate.1.both_ref), custom_call_target="tpu_custom_call" | custom-call | tf_op jit(solution)/shard_map/hand_on/pallas_call | solution.py:506

commit v5 on v4

--- a/solution.py
+++ b/solution.py
@@ -111,12 +111,14 @@
         r = resid_ref[:, cols]
         wr = w * r
         rows = stacked_rows(design_ref[0:HALF, cols], design_ref[HALF:WIDTH, cols], w, wr)
-        x = jnp.concatenate(rows, axis=0)
-        high = x.astype(jnp.bfloat16).astype(jnp.float32)
-        low = x - high
-        lhs = jnp.concatenate(
-            [high[0:EVEN], low[0:EVEN], high[EVEN:ROWS], low[EVEN:ROWS]], axis=0
-        ).astype(jnp.bfloat16)
+        lhs = []
+        for k in range(0, len(rows) - 1, 2):
+            x = jnp.concatenate(rows[k:k + 2], axis=0)
+            high = x.astype(jnp.bfloat16)
+            lhs += [high, (x - high.astype(jnp.float32)).astype(jnp.bfloat16)]
+        high = rows[-1].astype(jnp.bfloat16).astype(jnp.float32)
+        lhs.append(jnp.concatenate([high, rows[-1] - high], axis=0).astype(jnp.bfloat16))
+        lhs = jnp.concatenate(lhs, axis=0)
         unit = unit_ref[:, cols] - first_unit
         wrr = wr * r
         for k in range(TILE // LANES):
@@ -150,10 +152,12 @@
     tiles = []
     for n in range(len(accs[0])):
         both = pltpu.matmul_pop(accs[0][n]) + pltpu.matmul_pop(accs[1][n])
-        tiles.append(jnp.concatenate(
-            [both[0:EVEN] + both[EVEN:2 * EVEN], both[2 * EVEN:EVEN + ROWS] + both[EVEN + ROWS:]],
-            axis=0,
-        ))
+        sums = [
+            both[2 * k:2 * k + WIDTH] + both[2 * k + WIDTH:2 * k + 2 * WIDTH]
+            for k in range(0, EVEN, WIDTH)
+        ]
+        sums.append(both[2 * EVEN:EVEN + ROWS] + both[EVEN + ROWS:])
+        tiles.append(jnp.concatenate(sums, axis=0))
     return jnp.concatenate(tiles, axis=1)[:, 0:units]
 
 

time: 16.6 us -> 16.4 us (0.988)
  Pallas kernels: 15.2 us -> 15 us
    pallas_call x1, Pallas kernels: 2.86 us -> 2.65 us  [on_device(): pl.pallas_call(functools.partial(beyond, half, chunk), out_shape=(pltpu.V...]
where the time goes in v5:
time: 16.4 us; the launch traced here: 16.3 us
  Pallas kernels  15 us (91%)
  between operations  1.29 us (8%)
    pallas_call x1, Pallas kernels, on_device(): pl.pallas_call(functools.partial(kernel, n_tm, n_src, pieces), out_shape=...  11.7 us
    pallas_call x1, Pallas kernels, on_device(): pl.pallas_call(functools.partial(beyond, half, chunk), out_shape=(pltpu.V...  2.65 us
    pallas_call x1, Pallas kernels, on_device(): pl.pallas_call(hand_on, out_shape=(jax.ShapeDtypeStruct((own, WIDTH), jnp...  0.6 us

profile of v5, /device:TPU:0, one launch (start us, length us, event | category | flops | bytes accessed | tf_op | source)
XLA Modules:
  0.0 16.3 jit_solution(15210129618991439892)
XLA Ops:
  1.3 2.7 %beyond.1 = (f32[152,128]{1,0:T(8,128)S(1)}, f32[1,256]{1,0:T(1,128)S(1)}) custom-call(s32[1]{0:T(128)S(6)} %copy.8.count_ref, f32[16,16384]{1,0:T(8,128)} %design_hbm.3, s32[1,16384]{1,0:T(1,128)} %bitcast.6, f32[1,16384]{1,0:T(1,128)} %bitcast.8, f32[1,16384]{1,0:T(1,128)} %bitcast.10), custom_call_target="tpu_custom_call" | custom-call | tf_op jit(solution)/shard_map/beyond/pallas_call | solution.py:456
  3.9 11.7 %calibrate.1.both_ref = f32[8,128]{1,0:T(8,128)S(1)} custom-call(s32[1]{0:T(128)S(6)} %copy.8.count_ref, f32[16,16384]{1,0:T(8,128)} %design_hbm.3, s32[1,16384]{1,0:T(1,128)} %bitcast.7, f32[1,16384]{1,0:T(1,128)} %bitcast.9, f32[1,16384]{1,0:T(1,128)} %bitcast.11, f32[1,8]{1,0:T(1,128)} %bitcast.12, f32[152,128]{1,0:T(8,128)S(1)} %get-tuple-element.6.beyond_ref, ...), custom_call_target="tpu_custom_call" | custom-call | tf_op jit(solution)/shard_map/calibrate/pallas_call | solution.py:473
  15.7 0.6 %hand_on.1 = (f32[8,16]{1,0:T(8,128)}, f32[1,1]{1,0:T(1,128)}) custom-call(f32[8,128]{1,0:T(8,128)S(1)} %calibrate.1.both_ref), custom_call_target="tpu_custom_call" | custom-call | tf_op jit(solution)/shard_map/hand_on/pallas_call | solution.py:510

commit v6 on v5

--- a/solution.py
+++ b/solution.py
@@ -170,11 +170,16 @@
     )
 
 
+def arrived(bytes_ref, chunk, sem):
+    some = bytes_ref.at[:, pl.ds(0, (WIDTH + 3) * chunk)]
+    pltpu.make_async_copy(some, some, sem).wait()
+
+
 def beyond(
     start, chunk,
     count_ref, design_hbm, unit_hbm, resid_hbm, weight_hbm,
     sums_ref, weights_ref,
-    design_ref, unit_ref, resid_ref, weight_ref, load,
+    design_ref, unit_ref, resid_ref, weight_ref, bytes_ref, load,
 ):
     units = sums_ref.shape[1]
     slots = design_hbm.shape[1]
@@ -190,7 +195,7 @@
         far, here = arrays[which]
         size = pl.ds(pl.multiple_of(start + step * chunk, LANES), chunk)
         to = pl.ds(pl.multiple_of(step * chunk, LANES), chunk)
-        return pltpu.make_async_copy(far.at[:, size], here.at[:, to], load.at[step, which])
+        return pltpu.make_async_copy(far.at[:, size], here.at[:, to], load.at[step])
 
     def fetch_all(step, c):
         for which in range(4):
@@ -203,8 +208,7 @@
         zero = jnp.zeros((1, LANES), jnp.float32)
 
         def add(step, weights):
-            for which in range(4):
-                fetch(step, which).wait()
+            arrived(bytes_ref, chunk, load.at[step])
             return add_slots(
                 accs, (design_ref, unit_ref, resid_ref, weight_ref),
                 pl.multiple_of(step * chunk, LANES), chunk, first_unit, units, count - start, weights,
@@ -232,7 +236,7 @@
     out_ref,
     design_ref, unit_ref, resid_ref, weight_ref, damp_ref,
     sums_ref, kept_ref, extra, part, got, summed, spread, mine, heard, x_away, x_here,
-    load, small, send_a, recv_a, send_b, recv_b, send_c, recv_c,
+    bytes_ref, load, small, send_a, recv_a, send_b, recv_b, send_c, recv_c,
 ):
     tm, src = lax.axis_index("tm"), lax.axis_index("src")
     own = damp_ref.shape[1]
@@ -254,7 +258,7 @@
     def fetch(step, which):
         far, here = arrays[which]
         cols = pl.ds(starts[step], pieces[step])
-        return pltpu.make_async_copy(far.at[:, cols], here.at[:, cols], load.at[step, which])
+        return pltpu.make_async_copy(far.at[:, cols], here.at[:, cols], load.at[step])
 
     x_away[...] = jnp.zeros_like(x_away)
     damp_copy = pltpu.make_async_copy(damp_hbm, damp_ref, small)
@@ -288,8 +292,7 @@
         clear(accs)
         weights = weights_ref[:, 0:LANES], weights_ref[:, LANES:2 * LANES]
         for step in range(len(pieces)):
-            for which in range(4):
-                fetch(step, which).wait()
+            arrived(bytes_ref, pieces[step], load.at[step])
             weights = add_slots(
                 accs, (design_ref, unit_ref, resid_ref, weight_ref),
                 starts[step], pieces[step], first_unit, units, count, weights,
@@ -466,7 +469,8 @@
                 pltpu.VMEM((1, rest), jnp.int32),
                 pltpu.VMEM((1, rest), jnp.float32),
                 pltpu.VMEM((1, rest), jnp.float32),
-                pltpu.SemaphoreType.DMA((rest // chunk, 4)),
+                pltpu.VMEM((1, (WIDTH + 3) * chunk), jnp.float32),
+                pltpu.SemaphoreType.DMA((rest // chunk,)),
             ],
             name="beyond",
         )(obs_count, design, unit_index, residual, weight)
@@ -492,7 +496,8 @@
                 pltpu.VMEM((n_tm * n_solve, 1, LANES), jnp.float32),
                 pltpu.VMEM((lanes, LANES), jnp.float32),
                 pltpu.VMEM((own, LANES), jnp.float32),
-                pltpu.SemaphoreType.DMA((len(pieces), 4)),
+                pltpu.VMEM((1, (WIDTH + 3) * max(pieces)), jnp.float32),
+                pltpu.SemaphoreType.DMA((len(pieces),)),
             ] + [pltpu.SemaphoreType.DMA] * 7,
             compiler_params=pltpu.CompilerParams(collective_id=0, has_side_effects=True),
             name="calibrate",

time: 16.4 us -> 16.3 us (level)
  Pallas kernels: 15 us -> 14.8 us
where the time goes in v6:
time: 16.3 us; the launch traced here: 16.1 us
  Pallas kernels  14.8 us (91%)
  between operations  1.29 us (8%)
    pallas_call x1, Pallas kernels, on_device(): pl.pallas_call(functools.partial(kernel, n_tm, n_src, pieces), out_shape=...  11.7 us
    pallas_call x1, Pallas kernels, on_device(): pl.pallas_call(functools.partial(beyond, half, chunk), out_shape=(pltpu.V...  2.59 us
    pallas_call x1, Pallas kernels, on_device(): pl.pallas_call(hand_on, out_shape=(jax.ShapeDtypeStruct((own, WIDTH), jnp...  0.6 us

profile of v6, /device:TPU:0, one launch (start us, length us, event | category | flops | bytes accessed | tf_op | source)
XLA Modules:
  0.0 16.1 jit_solution(11886212213514704947)
XLA Ops:
  1.3 2.6 %beyond.1 = (f32[152,128]{1,0:T(8,128)S(1)}, f32[1,256]{1,0:T(1,128)S(1)}) custom-call(s32[1]{0:T(128)S(6)} %copy.8.count_ref, f32[16,16384]{1,0:T(8,128)} %design_hbm.3, s32[1,16384]{1,0:T(1,128)} %bitcast.6, f32[1,16384]{1,0:T(1,128)} %bitcast.8, f32[1,16384]{1,0:T(1,128)} %bitcast.10), custom_call_target="tpu_custom_call" | custom-call | tf_op jit(solution)/shard_map/beyond/pallas_call | solution.py:459
  3.9 11.7 %calibrate.1.both_ref = f32[8,128]{1,0:T(8,128)S(1)} custom-call(s32[1]{0:T(128)S(6)} %copy.8.count_ref, f32[16,16384]{1,0:T(8,128)} %design_hbm.3, s32[1,16384]{1,0:T(1,128)} %bitcast.7, f32[1,16384]{1,0:T(1,128)} %bitcast.9, f32[1,16384]{1,0:T(1,128)} %bitcast.11, f32[1,8]{1,0:T(1,128)} %bitcast.12, f32[152,128]{1,0:T(8,128)S(1)} %get-tuple-element.6.beyond_ref, ...), custom_call_target="tpu_custom_call" | custom-call | tf_op jit(solution)/shard_map/calibrate/pallas_call | solution.py:477
  15.5 0.6 %hand_on.1 = (f32[8,16]{1,0:T(8,128)}, f32[1,1]{1,0:T(1,128)}) custom-call(f32[8,128]{1,0:T(8,128)S(1)} %calibrate.1.both_ref), custom_call_target="tpu_custom_call" | custom-call | tf_op jit(solution)/shard_map/hand_on/pallas_call | solution.py:515

commit v7 on v6

--- a/solution.py
+++ b/solution.py
@@ -14,7 +14,10 @@
 EVEN = ROWS // WIDTH * WIDTH
 LANES = 128
 TILE = 256
+SHARE = 4
 FOLD = 4
+PACKED = (ROWS + HALF) // FOLD
+AUX = LANES // FOLD
 
 
 def pair_row(i, j):
@@ -91,16 +94,15 @@
         lax.fori_loop(0, n, lambda k, c: (body(k), c)[1], 0)
 
 
-def solved_by(n_src):
+def block_at(place, n_src):
     q = n_src // 4
-    blocks = []
-    for w in range(q + 1, n_src - q, 2):
-        away = -q if w < 2 * q else q
-        blocks.append((w, w - 1, w + away, w - 1 + away))
-    return blocks
-
-
-def add_slots(accs, refs, begin, chunk, first_unit, units, count, weights):
+    solver = q + 1 + 2 * (place // SHARE)
+    turn = place % SHARE
+    away = jnp.where(solver < 2 * q, -q, q)
+    return solver - turn % 2 + jnp.where(turn >= 2, away, 0)
+
+
+def add_slots(accs, refs, ids, begin, chunk, first_unit, count, weights):
     design_ref, unit_ref, resid_ref, weight_ref = refs
     chi, total = weights
     for t in range(chunk // TILE):
@@ -127,15 +129,21 @@
         q = t % 2
         for n, acc in enumerate(accs[q]):
             pltpu.matmul_push_rhs(
-                one_hot(unit, n, units), staging_register=0, mxu_index=q, transpose=True
+                one_hot(unit, n, ids), staging_register=0, mxu_index=q, transpose=True
             )
             pltpu.matmul_acc_lhs(acc, lhs, load_staged_rhs=0)
     return chi, total
 
 
-def one_hot(unit, n, units):
-    rows = min(units - n * TILE, TILE)
-    here = lax.broadcasted_iota(jnp.int16, (rows, TILE), 0) == (unit - n * TILE).astype(jnp.int16)
+def fill_ids(ids, own, n_src):
+    place = lax.broadcasted_iota(jnp.int32, ids.shape, 0)
+    unit = block_at(place // own, n_src) * own + place % own
+    ids[...] = unit.astype(jnp.int16)
+
+
+def one_hot(unit, n, ids):
+    rows = min(ids.shape[0] - n * TILE, TILE)
+    here = ids[pl.ds(n * TILE, rows), :] == unit.astype(jnp.int16)
     hot = jnp.where(here, jnp.bfloat16(1), jnp.bfloat16(0))
     if rows < TILE:
         hot = jnp.concatenate([hot, jnp.zeros((TILE - rows, TILE), jnp.bfloat16)], axis=0)
@@ -176,10 +184,10 @@
 
 
 def beyond(
-    start, chunk,
+    start, chunk, n_src,
     count_ref, design_hbm, unit_hbm, resid_hbm, weight_hbm,
     sums_ref, weights_ref,
-    design_ref, unit_ref, resid_ref, weight_ref, bytes_ref, load,
+    design_ref, unit_ref, resid_ref, weight_ref, ids, bytes_ref, load,
 ):
     units = sums_ref.shape[1]
     slots = design_hbm.shape[1]
@@ -210,13 +218,14 @@
         def add(step, weights):
             arrived(bytes_ref, chunk, load.at[step])
             return add_slots(
-                accs, (design_ref, unit_ref, resid_ref, weight_ref),
-                pl.multiple_of(step * chunk, LANES), chunk, first_unit, units, count - start, weights,
+                accs, (design_ref, unit_ref, resid_ref, weight_ref), ids,
+                pl.multiple_of(step * chunk, LANES), chunk, first_unit, count - start, weights,
             )
 
         @pl.when(turns > 0)
         def _():
             clear(accs)
+            fill_ids(ids, units // n_src, n_src)
             chi, total = lax.fori_loop(0, turns, add, (zero, zero))
             sums_ref[...] = drained(accs, units)
             weights_ref[:, 0:LANES] = chi
@@ -235,16 +244,15 @@
     count_ref, design_hbm, unit_hbm, resid_hbm, weight_hbm, damp_hbm, beyond_ref, weights_ref,
     out_ref,
     design_ref, unit_ref, resid_ref, weight_ref, damp_ref,
-    sums_ref, kept_ref, extra, part, got, summed, spread, mine, heard, x_away, x_here,
-    bytes_ref, load, small, send_a, recv_a, send_b, recv_b, send_c, recv_c,
+    sums_ref, kept_ref, part, got, summed, mine, heard, x_away, x_here,
+    ids, bytes_ref, load, small, send_a, recv_a, send_b, recv_b, send_c, recv_c,
 ):
     tm, src = lax.axis_index("tm"), lax.axis_index("src")
     own = damp_ref.shape[1]
     units = own * n_src
-    shares = solved_by(n_src)
-    n_solve = len(shares)
-    first_solver = shares[0][0]
-    lanes = own * n_src // n_solve
+    n_solve = n_src // SHARE
+    first_solver = n_src // 4 + 1
+    lanes = own * SHARE
     solves = (src >= first_solver) & (src < first_solver + 2 * n_solve) & (src % 2 == 1)
     rank = (src - first_solver) // 2
     up = src >= n_src // 2
@@ -287,6 +295,7 @@
 
     first_unit = tm * units
     count = count_ref[0]
+    fill_ids(ids, own, n_src)
 
     def body(accs):
         clear(accs)
@@ -294,8 +303,8 @@
         for step in range(len(pieces)):
             arrived(bytes_ref, pieces[step], load.at[step])
             weights = add_slots(
-                accs, (design_ref, unit_ref, resid_ref, weight_ref),
-                starts[step], pieces[step], first_unit, units, count, weights,
+                accs, (design_ref, unit_ref, resid_ref, weight_ref), ids,
+                starts[step], pieces[step], first_unit, count, weights,
             )
         sums_ref[...] = beyond_ref[...] + drained(accs, units)
         kept_ref[:, 0:LANES], kept_ref[:, LANES:2 * LANES] = weights
@@ -304,29 +313,22 @@
     sums = sums_ref[...]
     damp_copy.wait()
     damping = jnp.concatenate([damp_ref[...]] * n_src, axis=1)
-    block = lax.broadcasted_iota(jnp.int32, damping.shape, 1) // own
-    damping = jnp.where(block == src, damping, 0.0)
+    place = lax.broadcasted_iota(jnp.int32, damping.shape, 1) // own
+    damping = jnp.where(block_at(place, n_src) == src, damping, 0.0)
     fill = [jnp.zeros((1, units - LANES), jnp.float32)] if units > LANES else []
     chi = jnp.concatenate([kept_ref[:, 0:LANES]] + fill, axis=1)
     total = jnp.concatenate([kept_ref[:, LANES:2 * LANES]] + fill, axis=1)
-    left = jnp.concatenate(
-        [sums[LANES:ROWS], damping, chi, total,
-         jnp.zeros((2 * LANES - ROWS - 3, units), jnp.float32)], axis=0
-    )
-
-    def by_solver(rows):
-        return jnp.concatenate(
-            [rows[b * own:(b + 1) * own] for share in shares for b in share], axis=0
-        )
-
-    extra[...] = by_solver(jnp.transpose(left))
-    part[:, 0:lanes, :] = by_solver(jnp.transpose(sums[0:LANES])).reshape(n_solve, lanes, LANES)
-    packed = extra[pl.ds(0, units // FOLD, stride=FOLD), :]
-    lane = lax.broadcasted_iota(jnp.int32, packed.shape, 1) // (LANES // FOLD)
-    for b in range(1, FOLD):
-        more = extra[pl.ds(b, units // FOLD, stride=FOLD), :]
-        packed = jnp.where(lane == b, pltpu.roll(more, b * (LANES // FOLD), 1), packed)
-    part[:, lanes:, :] = packed.reshape(n_solve, lanes // FOLD, LANES)
+    none = jnp.zeros((FOLD * PACKED - ROWS - 3, units), jnp.float32)
+    rows = jnp.concatenate([sums, damping, chi, total, none], axis=0)
+    group = lax.broadcasted_iota(jnp.int32, (PACKED, LANES), 1) // AUX
+    for k in range(n_solve):
+        first = k * lanes // LANES * LANES
+        for g in range(FOLD):
+            more = rows[g * PACKED:(g + 1) * PACKED, first:first + LANES]
+            shift = (g * AUX - k * lanes) % LANES
+            more = pltpu.roll(more, shift, 1) if shift else more
+            message = jnp.where(group == g, more, message) if g else more
+        part[k] = message
 
     def send_to(k):
         pltpu.make_async_remote_copy(
@@ -370,15 +372,9 @@
         both = got[0]
         for p in range(1, n_src):
             both = both + got[p]
-        whole, ends = both[0:lanes], both[lanes:]
-        for a in range(lanes // FOLD):
-            for b in range(FOLD):
-                row = ends[a:a + 1]
-                spread[pl.ds(a * FOLD + b, 1), :] = (
-                    pltpu.roll(row, LANES - b * (LANES // FOLD), 1) if b else row
-                )
-        summed[0:LANES, :] = jnp.transpose(whole)
-        summed[LANES:2 * LANES, :] = jnp.transpose(spread[...])
+        for g in range(FOLD):
+            more = pltpu.roll(both, LANES - g * AUX, 1) if g else both
+            summed[pl.ds(g * PACKED, PACKED), :] = more[:, 0:lanes]
         damping, chi, total = (summed[pl.ds(ROWS + i, 1), :] for i in range(3))
         x, forward = solve(
             lambda i, j: summed[pl.ds(pair_row(i, j), 1), :],
@@ -447,8 +443,7 @@
         piece = half // 4 if half % 2048 == 0 else half
         pieces = (piece, half - piece) if half > piece else (half,)
         chunk = next(c for c in (4096, 2048, 1024, 512, 256) if (slots - half) % c == 0)
-        n_solve = len(solved_by(n_src))
-        lanes = units // n_solve
+        n_solve, lanes = n_src // SHARE, own * SHARE
         anywhere = pl.BlockSpec(memory_space=pl.ANY)
         vmem = pl.BlockSpec(memory_space=pltpu.VMEM)
         kept = lambda v: pltpu.with_memory_space_constraint(v, pltpu.VMEM)
@@ -457,7 +452,7 @@
         )
         rest = slots - half
         sums, weights = pl.pallas_call(
-            functools.partial(beyond, half, chunk),
+            functools.partial(beyond, half, chunk, n_src),
             out_shape=(
                 pltpu.VMEM((ROWS, units), jnp.float32),
                 pltpu.VMEM((1, 2 * LANES), jnp.float32),
@@ -469,6 +464,7 @@
                 pltpu.VMEM((1, rest), jnp.int32),
                 pltpu.VMEM((1, rest), jnp.float32),
                 pltpu.VMEM((1, rest), jnp.float32),
+                pltpu.VMEM((units, TILE), jnp.int16),
                 pltpu.VMEM((1, (WIDTH + 3) * chunk), jnp.float32),
                 pltpu.SemaphoreType.DMA((rest // chunk,)),
             ],
@@ -487,15 +483,14 @@
                 pltpu.VMEM((1, own), jnp.float32),
                 pltpu.VMEM((ROWS, units), jnp.float32),
                 pltpu.VMEM((1, 2 * LANES), jnp.float32),
-                pltpu.VMEM((units, LANES), jnp.float32),
-                pltpu.VMEM((n_solve, lanes + lanes // FOLD, LANES), jnp.float32),
-                pltpu.VMEM((n_src, lanes + lanes // FOLD, LANES), jnp.float32),
-                pltpu.VMEM((2 * LANES, lanes), jnp.float32),
-                pltpu.VMEM((lanes, LANES), jnp.float32),
+                pltpu.VMEM((n_solve, PACKED, LANES), jnp.float32),
+                pltpu.VMEM((n_src, PACKED, LANES), jnp.float32),
+                pltpu.VMEM((FOLD * PACKED, lanes), jnp.float32),
                 pltpu.VMEM((1, LANES), jnp.float32),
                 pltpu.VMEM((n_tm * n_solve, 1, LANES), jnp.float32),
                 pltpu.VMEM((lanes, LANES), jnp.float32),
                 pltpu.VMEM((own, LANES), jnp.float32),
+                pltpu.VMEM((units, TILE), jnp.int16),
                 pltpu.VMEM((1, (WIDTH + 3) * max(pieces)), jnp.float32),
                 pltpu.SemaphoreType.DMA((len(pieces),)),
             ] + [pltpu.SemaphoreType.DMA] * 7,

time: 16.3 us -> 16 us (0.982)
  Pallas kernels: 14.8 us -> 14.6 us
    pallas_call x1, Pallas kernels: 11.7 us -> 11.4 us  [on_device(): pl.pallas_call(functools.partial(kernel, n_tm, n_src, pieces), out_shape=...]
where the time goes in v7:
time: 16 us; the launch traced here: 15.9 us
  Pallas kernels  14.6 us (91%)
  between operations  1.29 us (8%)
    pallas_call x1, Pallas kernels, on_device(): pl.pallas_call(functools.partial(kernel, n_tm, n_src, pieces), out_shape=...  11.4 us
    pallas_call x1, Pallas kernels, on_device(): pl.pallas_call(functools.partial(beyond, half, chunk, n_src), out_shape=(...  2.61 us
    pallas_call x1, Pallas kernels, on_device(): pl.pallas_call(hand_on, out_shape=(jax.ShapeDtypeStruct((own, WIDTH), jnp...  0.6 us

profile of v7, /device:TPU:0, one launch (start us, length us, event | category | flops | bytes accessed | tf_op | source)
XLA Modules:
  0.0 15.9 jit_solution(3379814269220560708)
XLA Ops:
  1.3 2.6 %beyond.1 = (f32[152,128]{1,0:T(8,128)S(1)}, f32[1,256]{1,0:T(1,128)S(1)}) custom-call(s32[1]{0:T(128)S(6)} %copy.8.count_ref, f32[16,16384]{1,0:T(8,128)} %design_hbm.3, s32[1,16384]{1,0:T(1,128)} %bitcast.6, f32[1,16384]{1,0:T(1,128)} %bitcast.8, f32[1,16384]{1,0:T(1,128)} %bitcast.10), custom_call_target="tpu_custom_call" | custom-call | tf_op jit(solution)/shard_map/beyond/pallas_call | solution.py:454
  3.9 11.4 %calibrate.1.both_ref = f32[8,128]{1,0:T(8,128)S(1)} custom-call(s32[1]{0:T(128)S(6)} %copy.8.count_ref, f32[16,16384]{1,0:T(8,128)} %design_hbm.3, s32[1,16384]{1,0:T(1,128)} %bitcast.7, f32[1,16384]{1,0:T(1,128)} %bitcast.9, f32[1,16384]{1,0:T(1,128)} %bitcast.11, f32[1,8]{1,0:T(1,128)} %bitcast.12, f32[152,128]{1,0:T(8,128)S(1)} %get-tuple-element.6.beyond_ref, ...), custom_call_target="tpu_custom_call" | custom-call | tf_op jit(solution)/shard_map/calibrate/pallas_call | solution.py:473
  15.3 0.6 %hand_on.1 = (f32[8,16]{1,0:T(8,128)}, f32[1,1]{1,0:T(1,128)}) custom-call(f32[8,128]{1,0:T(8,128)S(1)} %calibrate.1.both_ref), custom_call_target="tpu_custom_call" | custom-call | tf_op jit(solution)/shard_map/hand_on/pallas_call | solution.py:510

commit v8 on v7

--- a/solution.py
+++ b/solution.py
@@ -172,7 +172,7 @@
 def with_sums(body, units):
     tiles = -(-units // TILE)
     shape = (2 * ROWS, TILE)
-    pl.run_scoped(
+    return pl.run_scoped(
         lambda *accs: body((accs[0:tiles], accs[tiles:2 * tiles])),
         *[pltpu.ACC(q)(shape, jnp.float32) for q in range(2) for _ in range(tiles)],
     )
@@ -244,7 +244,7 @@
     count_ref, design_hbm, unit_hbm, resid_hbm, weight_hbm, damp_hbm, beyond_ref, weights_ref,
     out_ref,
     design_ref, unit_ref, resid_ref, weight_ref, damp_ref,
-    sums_ref, kept_ref, part, got, summed, mine, heard, x_away, x_here,
+    part, got, summed, mine, heard, x_away, x_here,
     ids, bytes_ref, load, small, send_a, recv_a, send_b, recv_b, send_c, recv_c,
 ):
     tm, src = lax.axis_index("tm"), lax.axis_index("src")
@@ -306,18 +306,16 @@
                 accs, (design_ref, unit_ref, resid_ref, weight_ref), ids,
                 starts[step], pieces[step], first_unit, count, weights,
             )
-        sums_ref[...] = beyond_ref[...] + drained(accs, units)
-        kept_ref[:, 0:LANES], kept_ref[:, LANES:2 * LANES] = weights
-
-    with_sums(body, units)
-    sums = sums_ref[...]
+        return (beyond_ref[...] + drained(accs, units), *weights)
+
+    sums, chi, total = with_sums(body, units)
     damp_copy.wait()
     damping = jnp.concatenate([damp_ref[...]] * n_src, axis=1)
     place = lax.broadcasted_iota(jnp.int32, damping.shape, 1) // own
     damping = jnp.where(block_at(place, n_src) == src, damping, 0.0)
     fill = [jnp.zeros((1, units - LANES), jnp.float32)] if units > LANES else []
-    chi = jnp.concatenate([kept_ref[:, 0:LANES]] + fill, axis=1)
-    total = jnp.concatenate([kept_ref[:, LANES:2 * LANES]] + fill, axis=1)
+    chi = jnp.concatenate([chi] + fill, axis=1)
+    total = jnp.concatenate([total] + fill, axis=1)
     none = jnp.zeros((FOLD * PACKED - ROWS - 3, units), jnp.float32)
     rows = jnp.concatenate([sums, damping, chi, total, none], axis=0)
     group = lax.broadcasted_iota(jnp.int32, (PACKED, LANES), 1) // AUX
@@ -369,9 +367,10 @@
         repeat(n_solve - 1, lambda k: send_to(ranked(k, rank, n_solve, up)))
         got[src] = part[rank]
         wait_bytes(got, n_src - 1, recv_a)
-        both = got[0]
-        for p in range(1, n_src):
-            both = both + got[p]
+        each = [got[p] for p in range(n_src)]
+        while len(each) > 1:
+            each = [a + b for a, b in zip(each[::2], each[1::2])] + each[len(each) // 2 * 2:]
+        both = each[0]
         for g in range(FOLD):
             more = pltpu.roll(both, LANES - g * AUX, 1) if g else both
             summed[pl.ds(g * PACKED, PACKED), :] = more[:, 0:lanes]
@@ -383,7 +382,7 @@
         )
         terms = jnp.zeros_like(damping)
         squared = jnp.zeros_like(damping)
-        for i in range(WIDTH):
+        for i in reversed(range(WIDTH)):
             terms = terms + forward[i] * forward[i]
             squared = squared + x[i] * x[i]
         terms = terms + damping * squared
@@ -481,8 +480,6 @@
                 pltpu.VMEM((1, half), jnp.float32),
                 pltpu.VMEM((1, half), jnp.float32),
                 pltpu.VMEM((1, own), jnp.float32),
-                pltpu.VMEM((ROWS, units), jnp.float32),
-                pltpu.VMEM((1, 2 * LANES), jnp.float32),
                 pltpu.VMEM((n_solve, PACKED, LANES), jnp.float32),
                 pltpu.VMEM((n_src, PACKED, LANES), jnp.float32),
                 pltpu.VMEM((FOLD * PACKED, lanes), jnp.float32),

time: 16 us -> 16 us (level)
  no operation moved by 1% of the time
where the time goes in v8:
time: 16 us; the launch traced here: 15.9 us
  Pallas kernels  14.6 us (91%)
  between operations  1.29 us (8%)
    pallas_call x1, Pallas kernels, on_device(): pl.pallas_call(functools.partial(kernel, n_tm, n_src, pieces), out_shape=...  11.4 us
    pallas_call x1, Pallas kernels, on_device(): pl.pallas_call(functools.partial(beyond, half, chunk, n_src), out_shape=(...  2.61 us
    pallas_call x1, Pallas kernels, on_device(): pl.pallas_call(hand_on, out_shape=(jax.ShapeDtypeStruct((own, WIDTH), jnp...  0.6 us

profile of v8, /device:TPU:0, one launch (start us, length us, event | category | flops | bytes accessed | tf_op | source)
XLA Modules:
  0.0 15.9 jit_solution(13946505610720661218)
XLA Ops:
  1.3 2.6 %beyond.1 = (f32[152,128]{1,0:T(8,128)S(1)}, f32[1,256]{1,0:T(1,128)S(1)}) custom-call(s32[1]{0:T(128)S(6)} %copy.8.count_ref, f32[16,16384]{1,0:T(8,128)} %design_hbm.3, s32[1,16384]{1,0:T(1,128)} %bitcast.6, f32[1,16384]{1,0:T(1,128)} %bitcast.8, f32[1,16384]{1,0:T(1,128)} %bitcast.10), custom_call_target="tpu_custom_call" | custom-call | tf_op jit(solution)/shard_map/beyond/pallas_call | solution.py:453
  3.9 11.4 %calibrate.1.both_ref = f32[8,128]{1,0:T(8,128)S(1)} custom-call(s32[1]{0:T(128)S(6)} %copy.8.count_ref, f32[16,16384]{1,0:T(8,128)} %design_hbm.3, s32[1,16384]{1,0:T(1,128)} %bitcast.7, f32[1,16384]{1,0:T(1,128)} %bitcast.9, f32[1,16384]{1,0:T(1,128)} %bitcast.11, f32[1,8]{1,0:T(1,128)} %bitcast.12, f32[152,128]{1,0:T(8,128)S(1)} %get-tuple-element.6.beyond_ref, ...), custom_call_target="tpu_custom_call" | custom-call | tf_op jit(solution)/shard_map/calibrate/pallas_call | solution.py:472
  15.3 0.6 %hand_on.1 = (f32[8,16]{1,0:T(8,128)}, f32[1,1]{1,0:T(1,128)}) custom-call(f32[8,128]{1,0:T(8,128)S(1)} %calibrate.1.both_ref), custom_call_target="tpu_custom_call" | custom-call | tf_op jit(solution)/shard_map/hand_on/pallas_call | solution.py:507

commit v9 on v8

--- a/solution.py
+++ b/solution.py
@@ -319,7 +319,8 @@
     none = jnp.zeros((FOLD * PACKED - ROWS - 3, units), jnp.float32)
     rows = jnp.concatenate([sums, damping, chi, total, none], axis=0)
     group = lax.broadcasted_iota(jnp.int32, (PACKED, LANES), 1) // AUX
-    for k in range(n_solve):
+
+    def pack(k):
         first = k * lanes // LANES * LANES
         for g in range(FOLD):
             more = rows[g * PACKED:(g + 1) * PACKED, first:first + LANES]
@@ -334,6 +335,16 @@
             device_id={"tm": tm, "src": first_solver + 2 * k},
             device_id_type=pl.DeviceIdType.MESH,
         ).start()
+
+    pack(0)
+
+    @pl.when(jnp.logical_not(solves))
+    def _():
+        pl.semaphore_wait(barrier, n_solve)
+        send_to(0)
+
+    for k in range(1, n_solve):
+        pack(k)
 
     def wait_bytes(ref, n, sem):
         some = ref.at[pl.ds(0, n)]
@@ -402,8 +413,7 @@
 
     @pl.when(jnp.logical_not(solves))
     def _():
-        pl.semaphore_wait(barrier, n_solve)
-        repeat(n_solve, lambda k: send_to(jnp.where(up, k, n_solve - 1 - k)))
+        repeat(n_solve - 1, lambda k: send_to(k + 1))
         hand_over(0, src).wait_recv()
         out_ref[...] = x_here[...]
         wait_bytes(part, n_solve, send_a)

time: 16 us -> 16 us (level)
  no operation moved by 1% of the time
where the time goes in v9:
time: 16 us; the launch traced here: 15.9 us
  Pallas kernels  14.6 us (91%)
  between operations  1.29 us (8%)
    pallas_call x1, Pallas kernels, on_device(): pl.pallas_call(functools.partial(kernel, n_tm, n_src, pieces), out_shape=...  11.4 us
    pallas_call x1, Pallas kernels, on_device(): pl.pallas_call(functools.partial(beyond, half, chunk, n_src), out_shape=(...  2.61 us
    pallas_call x1, Pallas kernels, on_device(): pl.pallas_call(hand_on, out_shape=(jax.ShapeDtypeStruct((own, WIDTH), jnp...  0.6 us

profile of v9, /device:TPU:0, one launch (start us, length us, event | category | flops | bytes accessed | tf_op | source)
XLA Modules:
  0.0 15.9 jit_solution(6264880914840872898)
XLA Ops:
  1.3 2.6 %beyond.1 = (f32[152,128]{1,0:T(8,128)S(1)}, f32[1,256]{1,0:T(1,128)S(1)}) custom-call(s32[1]{0:T(128)S(6)} %copy.8.count_ref, f32[16,16384]{1,0:T(8,128)} %design_hbm.3, s32[1,16384]{1,0:T(1,128)} %bitcast.6, f32[1,16384]{1,0:T(1,128)} %bitcast.8, f32[1,16384]{1,0:T(1,128)} %bitcast.10), custom_call_target="tpu_custom_call" | custom-call | tf_op jit(solution)/shard_map/beyond/pallas_call | solution.py:463
  3.9 11.4 %calibrate.1.both_ref = f32[8,128]{1,0:T(8,128)S(1)} custom-call(s32[1]{0:T(128)S(6)} %copy.8.count_ref, f32[16,16384]{1,0:T(8,128)} %design_hbm.3, s32[1,16384]{1,0:T(1,128)} %bitcast.7, f32[1,16384]{1,0:T(1,128)} %bitcast.9, f32[1,16384]{1,0:T(1,128)} %bitcast.11, f32[1,8]{1,0:T(1,128)} %bitcast.12, f32[152,128]{1,0:T(8,128)S(1)} %get-tuple-element.6.beyond_ref, ...), custom_call_target="tpu_custom_call" | custom-call | tf_op jit(solution)/shard_map/calibrate/pallas_call | solution.py:482
  15.3 0.6 %hand_on.1 = (f32[8,16]{1,0:T(8,128)}, f32[1,1]{1,0:T(1,128)}) custom-call(f32[8,128]{1,0:T(8,128)S(1)} %calibrate.1.both_ref), custom_call_target="tpu_custom_call" | custom-call | tf_op jit(solution)/shard_map/hand_on/pallas_call | solution.py:517

commit v10 on v9

--- a/solution.py
+++ b/solution.py
@@ -449,9 +449,8 @@
         units = own * n_src
         slots = design.shape[1]
         half = slots // 2
-        piece = half // 4 if half % 2048 == 0 else half
-        pieces = (piece, half - piece) if half > piece else (half,)
-        chunk = next(c for c in (4096, 2048, 1024, 512, 256) if (slots - half) % c == 0)
+        pieces = (half,)
+        chunk = next(c for c in (8192, 4096, 2048, 1024, 512, 256) if (slots - half) % c == 0)
         n_solve, lanes = n_src // SHARE, own * SHARE
         anywhere = pl.BlockSpec(memory_space=pl.ANY)
         vmem = pl.BlockSpec(memory_space=pltpu.VMEM)

time: 16 us -> 16 us (level)
  no operation moved by 1% of the time
where the time goes in v10:
time: 16 us; the launch traced here: 15.9 us
  Pallas kernels  14.6 us (91%)
  between operations  1.29 us (8%)
    pallas_call x1, Pallas kernels, on_device(): pl.pallas_call(functools.partial(kernel, n_tm, n_src, pieces), out_shape=...  11.4 us
    pallas_call x1, Pallas kernels, on_device(): pl.pallas_call(functools.partial(beyond, half, chunk, n_src), out_shape=(...  2.58 us
    pallas_call x1, Pallas kernels, on_device(): pl.pallas_call(hand_on, out_shape=(jax.ShapeDtypeStruct((own, WIDTH), jnp...  0.6 us

profile of v10, /device:TPU:0, one launch (start us, length us, event | category | flops | bytes accessed | tf_op | source)
XLA Modules:
  0.0 15.9 jit_solution(9735563010567617749)
XLA Ops:
  1.3 2.6 %beyond.1 = (f32[152,128]{1,0:T(8,128)S(1)}, f32[1,256]{1,0:T(1,128)S(1)}) custom-call(s32[1]{0:T(128)S(6)} %copy.8.count_ref, f32[16,16384]{1,0:T(8,128)} %design_hbm.3, s32[1,16384]{1,0:T(1,128)} %bitcast.6, f32[1,16384]{1,0:T(1,128)} %bitcast.8, f32[1,16384]{1,0:T(1,128)} %bitcast.10), custom_call_target="tpu_custom_call" | custom-call | tf_op jit(solution)/shard_map/beyond/pallas_call | solution.py:462
  3.9 11.4 %calibrate.1.both_ref = f32[8,128]{1,0:T(8,128)S(1)} custom-call(s32[1]{0:T(128)S(6)} %copy.8.count_ref, f32[16,16384]{1,0:T(8,128)} %design_hbm.3, s32[1,16384]{1,0:T(1,128)} %bitcast.7, f32[1,16384]{1,0:T(1,128)} %bitcast.9, f32[1,16384]{1,0:T(1,128)} %bitcast.11, f32[1,8]{1,0:T(1,128)} %bitcast.12, f32[152,128]{1,0:T(8,128)S(1)} %get-tuple-element.6.beyond_ref, ...), custom_call_target="tpu_custom_call" | custom-call | tf_op jit(solution)/shard_map/calibrate/pallas_call | solution.py:481
  15.3 0.6 %hand_on.1 = (f32[8,16]{1,0:T(8,128)}, f32[1,1]{1,0:T(1,128)}) custom-call(f32[8,128]{1,0:T(8,128)S(1)} %calibrate.1.both_ref), custom_call_target="tpu_custom_call" | custom-call | tf_op jit(solution)/shard_map/hand_on/pallas_call | solution.py:516
